TPU v7x, 32 devices: a whole 2x2x4 slice. The times are simulated.
32 devices in a mesh: expert: 16 (over z, y, x), etp: 2 (over core).
Axes of the slice: x: 2, y: 2, z: 4, core: 2. Of those that a mesh axis runs over, the one named last changes fastest.
Arguments:
- grad_out: bfloat16 [2048, 3584], P('expert', 'etp'), may hold values from -6 to 6
- combine: bfloat16 [2048, 8], P('expert'), may hold values from 0.099609375 to 2.5
- expert_ids: int32 [2048, 8], P('expert'), may hold values from 0 to 31, all different within a row; in each aligned block of 128 rows (0 to 127, 128 to 255, ...) at most 64 rows name the same one
- saved_gate: bfloat16 [1024, 32, 1024], P(None, 'expert', 'etp'), may hold values from -6 to 6
- saved_up: bfloat16 [1024, 32, 1024], P(None, 'expert', 'etp'), may hold values from -1.5 to 1.5
- gate_weight: bfloat16 [32, 3584, 1024], P('expert', None, 'etp'), may hold values from -0.09375 to 0.09375
- up_weight: bfloat16 [32, 3584, 1024], P('expert', None, 'etp'), may hold values from -0.09375 to 0.09375
- down_weight: bfloat16 [32, 1024, 3584], P('expert', 'etp'), may hold values from -0.09375 to 0.09375
Outputs:
- grad_tokens: bfloat16 [2048, 3584], P('expert', 'etp')
- grad_combine: bfloat16 [2048, 8], P('expert')
Inputs may be any that keep to these rules, and one draw needn't show every extreme that they name: `expert_ids`: each token names 8 different experts. Among the 128 tokens of one block (one index of expert), at most 64 name any one expert, and some blocks reach that bound.
All inputs are finite; a program needn't handle non-finite values.
Results may differ from a plain program's by a relative error of at most 0.012.
Values may be sent and summed in bfloat16 or wider, within the bound.
A program may use at most 192 MiB of HBM per device.

v0:
```python
import jax
import jax.numpy as jnp
from jax import lax
from jax.sharding import PartitionSpec as P


def on_device(
    grad_out, combine, expert_ids, saved_gate, saved_up, gate_weight, up_weight, down_weight
):
    groups = lax.axis_size("expert")
    per_group = gate_weight.shape[0]
    tokens = grad_out.shape[0]
    capacity = saved_gate.shape[0] // groups
    hidden = saved_gate.shape[2]
    experts = groups * per_group
    chosen = expert_ids[:, :, None] == jnp.arange(experts, dtype=jnp.int32)[None, None, :]
    weights = jnp.sum(jnp.where(chosen, combine[:, :, None].astype(jnp.float32), 0.0), axis=1)
    weights = weights.astype(jnp.bfloat16).reshape(tokens, groups, per_group)
    weights = lax.all_to_all(
        weights.transpose(1, 2, 0), "expert", split_axis=0, concat_axis=0, tiled=True
    )
    rows = lax.all_gather(grad_out, "expert", axis=0, tiled=True)
    rows = lax.all_gather(rows, "etp", axis=1, tiled=True)
    rows = rows.reshape(groups, tokens, -1)
    named = (weights > 0).astype(jnp.float32)
    position = jnp.cumsum(named, axis=2) - named
    slot = jnp.where(named > 0, position, -1.0)
    select = slot[:, :, None, :] == jnp.arange(capacity, dtype=jnp.float32)[None, None, :, None]
    scale = jnp.sum(jnp.where(select, weights[:, :, None, :].astype(jnp.float32), 0.0), axis=3)
    scale = scale.transpose(1, 0, 2)[..., None]
    select = select.astype(jnp.bfloat16)
    slot_rows = jnp.einsum(
        "blct,btd->lbcd", select, rows, preferred_element_type=jnp.bfloat16
    )
    grad_hidden = jnp.einsum(
        "lbcd,lfd->lbcf", slot_rows, down_weight, preferred_element_type=jnp.float32
    )
    gate_value = saved_gate.reshape(groups, capacity, per_group, hidden).transpose(2, 0, 1, 3)
    up_value = saved_up.reshape(groups, capacity, per_group, hidden).transpose(2, 0, 1, 3)
    gate_value = gate_value.astype(jnp.float32)
    up_value = up_value.astype(jnp.float32)
    gate_sigmoid = jax.nn.sigmoid(gate_value)
    activated = gate_value * gate_sigmoid
    weight_part = jnp.sum(grad_hidden * activated * up_value, axis=3)
    scaled = scale * grad_hidden
    grad_gate = (
        scaled * up_value * gate_sigmoid * (1.0 + gate_value * (1.0 - gate_sigmoid))
    ).astype(jnp.bfloat16)
    grad_up = (scaled * activated).astype(jnp.bfloat16)
    weight_tok = jnp.einsum(
        "blct,lbc->blt", select, weight_part.astype(jnp.bfloat16),
        preferred_element_type=jnp.float32,
    ).astype(jnp.bfloat16)
    weight_tok = lax.psum(weight_tok, "etp")
    weight_tok = lax.all_to_all(weight_tok, "expert", split_axis=0, concat_axis=0, tiled=True)
    weight_tok = weight_tok.transpose(2, 0, 1).reshape(tokens, 1, experts)
    grad_combine = jnp.sum(
        jnp.where(chosen, weight_tok.astype(jnp.float32), 0.0), axis=2
    ).astype(jnp.bfloat16)
    partial = jnp.einsum(
        "lbcf,ldf->lbcd", grad_gate, gate_weight, preferred_element_type=jnp.float32
    )
    partial = partial + jnp.einsum(
        "lbcf,ldf->lbcd", grad_up, up_weight, preferred_element_type=jnp.float32
    )
    partial = jnp.einsum(
        "blct,lbcd->btd", select, partial.astype(jnp.bfloat16),
        preferred_element_type=jnp.float32,
    ).astype(jnp.bfloat16)
    partial = partial.reshape(groups * tokens, -1)
    partial = lax.psum_scatter(partial, "etp", scatter_dimension=1, tiled=True)
    grad_tokens = lax.psum_scatter(partial, "expert", scatter_dimension=0, tiled=True)
    return (grad_tokens, grad_combine)


def solution(mesh):
    in_specs = (
        P("expert", "etp"),
        P("expert", None),
        P("expert", None),
        P(None, "expert", "etp"),
        P(None, "expert", "etp"),
        P("expert", None, "etp"),
        P("expert", None, "etp"),
        P("expert", "etp", None),
    )
    out_specs = (P("expert", "etp"), P("expert", None))
    return jax.shard_map(
        on_device, mesh=mesh, in_specs=in_specs, out_specs=out_specs, check_vma=False
    )
```

profile of v0, /device:TPU:0, one launch (start us, length us, event | category | flops | bytes accessed | tf_op | source)
XLA Modules:
  0.0 412.5 jit_solution(12846402701796683711)
XLA Ops:
  7.2 0.0 copy-start.3
  7.2 0.0 copy-start.2
  7.2 0.0 copy-start
  7.2 0.0 all-gather.3.cloned.1.call-start
  7.2 0.7 all-gather.3.cloned.1.call-update
  7.9 0.0 all-gather.5.cloned.1.call-start
  8.0 108.3 %all-gather.3.cloned.1.call-done = bf16[2048,1792]{1,0:T(8,128)(2,1)} async-done(((bf16[128,1792]{1,0:T(8,128)(2,1)}), bf16[2048,1792]{1,0:T(8,128)(2,1)}) %all-gather.3.cloned.1.call-update) | async-done | bytes 7340048 | tf_op jit(solution)/shard_map/all_gather | solution.py:22
  116.3 0.0 all-gather.5.cloned.1.call-update
  116.3 0.0 copy-done.3
  116.3 0.0 copy-done.2
  116.3 0.6 select_reduce_fusion.2
  117.0 3.9 all-to-all-start
  120.9 0.0 reduce-scatter.3.cloned.1.call-start
  121.0 0.0 copy-done
  121.0 3.1 copy.40
  124.1 0.0 copy-start.1
  124.1 4.2 %convert_element_type.97 = f32[1024,2,512]{2,1,0:T(2,128)} convert(bf16[1024,2,512]{2,1,0:T(2,128)(2,1)S(1)} %copy-done) | non-fusion elementwise | flops 1048576 | bytes 6291456 | tf_op jit(solution)/shard_map/convert_element_type | solution.py:40
  128.2 0.0 copy-done.1
  128.2 2.9 copy.39
  131.2 3.9 convert_element_type.96
  135.1 0.0 all-to-all-done
  135.1 0.8 reduce_window_sum.11
  135.9 0.4 select_reduce_fusion
  136.3 6.9 %all-gather.5.cloned.1.call-done = bf16[2048,3584]{1,0:T(8,128)(2,1)} async-done(((bf16[2048,1792]{1,0:T(8,128)(2,1)}), bf16[2048,3584]{1,0:T(8,128)(2,1)}) %all-gather.5.cloned.1.call-update) | async-done | bytes 14680080 | tf_op jit(solution)/shard_map/all_gather | solution.py:23
  143.2 21.5 %multiply_convert_fusion = (bf16[2,16,64,512]{3,2,1,0:T(8,128)(2,1)}, bf16[2,16,64,512]{3,2,1,0:T(8,128)(2,1)}, bf16[2,16,64]{2,1,0:T(8,128)(2,1)S(1)}) fusion(f32[2,16,64]{2,1,0:T(8,128)S(1)} %copy.37, f32[1024,2,512]{2,1,0:T(2,128)} %convert_element_type.97, f32[1024,2,512]{2,1,0:T(2,128)} %convert_element_type.96, f32[2,16,64,512]{3,2,1,0:T(8,128)} %bitcast.49, ...), kind=kOutput, calls=%fused_computation.12 | convolution fusion | flops 9417521152 | bytes 43020288 | tf_op jit(solution)/shard_map/lbcd,lfd->lbcf/dot_general | solution.py:35
  164.7 0.0 copy-start.4
  164.7 16.4 %fusion.6 = f32[2,16,64,3584]{3,2,0,1:T(8,128)} fusion(bf16[2,3584,512]{2,1,0:T(8,128)(2,1)} %param.14, bf16[2,16,64,512]{3,2,1,0:T(8,128)(2,1)} %get-tuple-element.2), kind=kOutput, calls=%fused_computation.7 | convolution fusion | flops 7516192768 | bytes 38797312 | tf_op jit(solution)/shard_map/lbcf,ldf->lbcd/dot_general | solution.py:63
  181.1 0.0 copy-done.4
  181.1 16.6 %fusion.8 = f32[2,16,64,3584]{3,2,0,1:T(8,128)} fusion(bf16[2,3584,512]{2,1,0:T(8,128)(2,1)} %param.13, bf16[2,16,64,512]{3,2,1,0:T(8,128)(2,1)S(1)} %copy-done.4), kind=kOutput, calls=%fused_computation.9 | convolution fusion | flops 7516192768 | bytes 38797312 | tf_op jit(solution)/shard_map/lbcf,ldf->lbcd/dot_general | solution.py:60
  197.7 25.0 %bitcast_convert_fusion = bf16[16,128,3584]{2,1,0:T(8,128)(2,1)} fusion(f32[2,16,64,3584]{3,2,0,1:T(8,128)} %fusion.8, f32[2,16,64,3584]{3,2,0,1:T(8,128)} %fusion.6, f32[16,2,128]{2,1,0:T(2,128)S(1)} %copy.36), kind=kOutput, calls=%fused_computation | convolution fusion | flops 1901330432 | bytes 73416704 | tf_op jit(solution)/shard_map/blct,lbcd->btd/dot_general | solution.py:66
  222.7 0.0 reduce-scatter.3.cloned.1.call-update
  222.7 0.0 reduce-scatter.5.cloned.1.call-start
  222.8 22.2 %reduce-scatter.3.cloned.1.call-done = bf16[2048,1792]{1,0:T(8,128)(2,1)} async-done(((bf16[2048,3584]{1,0:T(8,128)(2,1)}), bf16[2048,1792]{1,0:T(8,128)(2,1)}) %reduce-scatter.3.cloned.1.call-update) | async-done | bytes 7340048 | tf_op jit(solution)/shard_map/reduce_scatter | solution.py:71
  245.0 0.0 reduce-scatter.5.cloned.1.call-update
  245.0 0.3 fusion.15
  245.3 2.5 psum.7
  247.8 14.0 %all_to_all.10 = bf16[16,2,128]{2,1,0:T(2,128)(2,1)S(1)} all-to-all(bf16[16,2,128]{2,1,0:T(2,128)(2,1)S(1)} %psum.7), channel_id=1, replica_groups=mesh['expert'=16,'etp'=2] {'expert'}, dimensions={0} | all-to-all | bytes 16384 | tf_op jit(solution)/shard_map/all_to_all | solution.py:55
  261.9 0.6 select_reduce_fusion.1
  262.5 143.5 %reduce-scatter.5.cloned.1.call-done = bf16[128,1792]{1,0:T(8,128)(2,1)} async-done(((bf16[2048,1792]{1,0:T(8,128)(2,1)}), bf16[128,1792]{1,0:T(8,128)(2,1)}) %reduce-scatter.5.cloned.1.call-update) | async-done | bytes 458768 | tf_op jit(solution)/shard_map/reduce_scatter | solution.py:72
  (8 shorter events, 0.1 us)
Async XLA Ops:
  7.2 109.1 %copy-start.3 = (bf16[128,8]{0,1:T(8,128)(2,1)S(1)}, bf16[128,8]{0,1:T(8,128)(2,1)}, u32[]{:S(2)}) copy-start(bf16[128,8]{0,1:T(8,128)(2,1)} %param.9) | copy-start | bytes 6148
  7.2 109.2 %copy-start.2 = (s32[128,8]{0,1:T(8,128)S(1)}, s32[128,8]{0,1:T(8,128)}, u32[]{:S(2)}) copy-start(s32[128,8]{0,1:T(8,128)} %param.10) | copy-start | bytes 12292
  7.2 113.8 %copy-start = (bf16[1024,2,512]{2,1,0:T(2,128)(2,1)S(1)}, bf16[1024,2,512]{2,1,0:T(2,128)(2,1)}, u32[]{:S(2)}) copy-start(bf16[1024,2,512]{2,1,0:T(2,128)(2,1)} %param.11) | copy-start | bytes 6291460
  7.2 109.1 %all-gather.3.cloned.1.call-start = ((), (), s32[]{:S(2)}) async-start(), calls=%async_computation.4 | async-start | bytes 7798784 | tf_op jit(solution)/shard_map/all_gather | solution.py:22
  7.9 135.3 %all-gather.5.cloned.1.call-start = ((), (), s32[]{:S(2)}) async-start(), calls=%async_computation.5 | async-start | bytes 22020096 | tf_op jit(solution)/shard_map/all_gather | solution.py:23
  117.0 18.1 %all-to-all-start = ((bf16[16,2,128]{2,1,0:T(2,128)(2,1)}), bf16[16,2,128]{2,1,0:T(2,128)(2,1)S(1)}, u32[]{:S(2)}, u32[]{:S(2)}) async-start(bf16[16,2,128]{2,1,0:T(2,128)(2,1)} %bitcast.1), calls=%async_computation | async-start | bytes 16384 | tf_op jit(solution)/shard_map/all_to_all | solution.py:19
  120.9 124.1 %reduce-scatter.3.cloned.1.call-start = ((), (), s32[]{:S(2)}) async-start(), calls=%async_computation.6 | async-start | bytes 22020096 | tf_op jit(solution)/shard_map/reduce_scatter | solution.py:71
  124.1 4.2 %copy-start.1 = (bf16[1024,2,512]{2,1,0:T(2,128)(2,1)S(1)}, bf16[1024,2,512]{2,1,0:T(2,128)(2,1)}, u32[]{:S(2)}) copy-start(bf16[1024,2,512]{2,1,0:T(2,128)(2,1)} %param.12) | copy-start | bytes 6291460
  164.7 16.4 %copy-start.4 = (bf16[2,16,64,512]{3,2,1,0:T(8,128)(2,1)S(1)}, bf16[2,16,64,512]{3,2,1,0:T(8,128)(2,1)}, u32[]{:S(2)}) copy-start(bf16[2,16,64,512]{3,2,1,0:T(8,128)(2,1)} %get-tuple-element.3) | copy-start | bytes 6291460
  222.7 183.2 %reduce-scatter.5.cloned.1.call-start = ((), (), s32[]{:S(2)}) async-start(), calls=%async_computation.7 | async-start | bytes 7798784 | tf_op jit(solution)/shard_map/reduce_scatter | solution.py:72
Sparse Core Ops, SparseCore 0:
  10.7 105.5 all-gather.2
  117.8 25.3 all-gather.4
  222.8 22.1 reduce-scatter.2
  247.7 158.1 reduce-scatter.4
where the time goes:
time: 414 us; the launch traced here: 412 us
  waiting for transfers between devices  282 us (68%)
  matrix products  79.7 us (19%)
  blocking collectives  16.6 us (4%)
  between operations  13.9 us (3%)
  other arithmetic  10.5 us (3%)
  local copies, waits for them, and re-layouts  6.05 us (1%)
    reduce_scatter x1, waiting for transfers between devices, on_device(): lax.psum_scatter(partial, 'expert', scatter_dimension=0, tiled=True)  143 us
    all_gather x1, waiting for transfers between devices, on_device(): rows = lax.all_gather(grad_out, 'expert', axis=0, tiled=True)  108 us
    dot_general x1, matrix products, on_device(): jnp.einsum('blct,lbcd->btd', select, partial.astype(jnp.bfloat16), prefer...  25 us
    reduce_scatter x1, waiting for transfers between devices, on_device(): partial = lax.psum_scatter(partial, 'etp', scatter_dimension=1, tiled=True)  22.2 us
    dot_general x1, matrix products, on_device(): jnp.einsum('lbcd,lfd->lbcf', slot_rows, down_weight, preferred_element_ty...  21.5 us
    dot_general x1, matrix products, on_device(): jnp.einsum('lbcf,ldf->lbcd', grad_gate, gate_weight, preferred_element_ty...  16.6 us
    dot_general x1, matrix products, on_device(): jnp.einsum('lbcf,ldf->lbcd', grad_up, up_weight, preferred_element_type=j...  16.4 us
    all_to_all x1, blocking collectives, on_device(): lax.all_to_all(weight_tok, 'expert', split_axis=0, concat_axis=0, tiled=T...  14 us
  transfers between devices with their start and end apart: 5, of which 4 were waited for; matrix products, arithmetic and copies ran while one was open for 4% of the time, Pallas kernels for 0%

commit v1 on v0

--- a/solution.py
+++ b/solution.py
@@ -1,10 +1,611 @@
+import functools
+
 import jax
 import jax.numpy as jnp
 from jax import lax
+from jax.experimental import pallas as pl
+from jax.experimental.pallas import tpu as pltpu
 from jax.sharding import PartitionSpec as P
 
-
-def on_device(
+MESH = pl.DeviceIdType.MESH
+VMEM_LIMIT = 66_000_000
+TOKEN_BYTES = 24 * 2**20
+NT = (((1,), (1,)), ((), ()))
+TN = (((0,), (0,)), ((), ()))
+ROWS = 8
+
+
+def dot_nt(a, b):
+    return lax.dot_general(a, b, NT, preferred_element_type=jnp.float32)
+
+
+def place():
+    e = lax.axis_index("expert")
+    c = lax.axis_index("etp")
+    return e, c, e // 4, (e // 2) % 2, e % 2
+
+
+def index(z, y, x):
+    return z * 4 + y * 2 + x
+
+
+def enter(groups, e, c):
+    barrier = pltpu.get_barrier_semaphore()
+
+    @pl.loop(1, groups)
+    def _(i):
+        pl.semaphore_signal(
+            barrier, inc=1, device_id=(lax.rem(e + i, groups), c), device_id_type=MESH
+        )
+
+    pl.semaphore_signal(barrier, inc=1, device_id=(e, 1 - c), device_id_type=MESH)
+    pl.semaphore_wait(barrier, groups)
+
+
+def remote(src, dst, send, recv, expert, core):
+    return pltpu.make_async_remote_copy(
+        src_ref=src,
+        dst_ref=dst,
+        send_sem=send,
+        recv_sem=recv,
+        device_id=(expert, core),
+        device_id_type=MESH,
+    )
+
+
+def one_hot(slot_row, capacity):
+    tokens = slot_row.shape[1]
+    at = lax.broadcasted_iota(jnp.int32, (capacity, tokens), 0).astype(jnp.float32)
+    return jnp.where(slot_row == at, 1.0, 0.0)
+
+
+def dispatch_kernel(
+    nz, capacity,
+    x_hbm, weights_ref, down_hbm, gate_ref, up_ref,
+    hidden_ref, slot_ref, part_ref,
+    own, other, weights, down, rows_own, rows_other, scale,
+    load_sem, sx, rx, sy, ry, su, sd, rz, sc, rc, sw, rw,
+):
+    e, c, z, y, x = place()
+    groups = nz * 4
+    per_group, hidden, _ = down.shape
+    tokens = weights.shape[2]
+    features = own.shape[3]
+    half = tokens // 2
+    width = 256
+    pieces = hidden // width
+    beside, above = index(z, y, 1 - x), index(z, 1 - y, x)
+
+    load_x = pltpu.make_async_copy(x_hbm, own.at[e], load_sem.at[0])
+    load_x.start()
+    load_down = pltpu.make_async_copy(down_hbm, down, load_sem.at[1])
+    load_down.start()
+    weights[e] = weights_ref[e]
+    enter(groups, e, c)
+    load_x.wait()
+
+    def along_x(b, h, p, slot):
+        return remote(own.at[b, h], own.at[b, h], sx.at[p, slot], rx.at[p, slot], beside, c)
+
+    def along_y(b, h, p, slot):
+        return remote(own.at[b, h], own.at[b, h], sy.at[p, slot], ry.at[p, slot], above, c)
+
+    def along_z(p, h, up):
+        b = index(p, y, x)
+        to = e + 4 if up else e - 4
+        return remote(own.at[b, h], own.at[b, h], (su if up else sd).at[p, h], rz.at[p, h], to, c)
+
+    def cross(b):
+        return remote(own.at[b], other.at[b], sc.at[b], rc.at[b], e, 1 - c)
+
+    def plane_send(p):
+        b = index(p, y, x)
+        along_x(b, 0, p, 0).start()
+        along_y(b, 1, p, 1).start()
+        along_x(b, 1, p, 1).start()
+        along_y(b, 0, p, 0).start()
+
+    def order(k):
+        low = jnp.where(k <= z, z - k, k)
+        back = nz - 1 - z
+        high = jnp.where(k <= back, z + k, nz - 1 - k)
+        return jnp.where(z < nz // 2, low, high)
+
+    plane_send(z)
+
+    @pl.when(z < nz - 1)
+    def _():
+        for h in range(2):
+            along_z(z, h, True).start()
+
+    @pl.when(z > 0)
+    def _():
+        for h in range(2):
+            along_z(z, h, False).start()
+
+    cross(e).start()
+
+    def tile(i):
+        to = lax.rem(e + i, groups)
+        return remote(weights_ref.at[to], weights.at[e], sw.at[i], rw.at[i], to, c)
+
+    @pl.loop(1, groups)
+    def _(i):
+        tile(i).start()
+
+    @pl.loop(1, groups)
+    def _(i):
+        tile(i).wait_recv()
+
+    named = (weights[...] > 0).astype(jnp.bfloat16).reshape(groups * ROWS, tokens)
+    first = lax.broadcasted_iota(jnp.int32, (tokens, tokens), 0)
+    second = lax.broadcasted_iota(jnp.int32, (tokens, tokens), 1)
+    before = (first < second).astype(jnp.bfloat16)
+    position = jnp.dot(named, before, preferred_element_type=jnp.float32)
+    slot_ref[...] = jnp.where(named > 0, position, -1.0).reshape(groups, ROWS, tokens)
+    part_ref[...] = jnp.zeros_like(part_ref)
+    load_down.wait()
+
+    own_at = pl.multiple_of(c * features, 128)
+    other_at = pl.multiple_of((1 - c) * features, 128)
+
+    def gather(b, q):
+        slots = slot_ref[b]
+        table = weights[b]
+        picks = []
+        for l in range(per_group):
+            pick = one_hot(slots[l : l + 1], capacity)
+            amount = jnp.sum(pick * table[l : l + 1], axis=1, keepdims=True)
+            scale[l, pl.ds(q * capacity, capacity)] = jnp.broadcast_to(amount, (capacity, 128))
+            picks.append(pick)
+        pick = jnp.concatenate(picks, axis=0).astype(jnp.bfloat16)
+        for held, rows in ((own, rows_own), (other, rows_other)):
+            block = held[b].reshape(tokens, features)
+            got = jnp.dot(pick, block, preferred_element_type=jnp.float32).astype(jnp.bfloat16)
+            for l in range(per_group):
+                rows[l, pl.ds(q * capacity, capacity)] = got[l * capacity : (l + 1) * capacity]
+
+    def hidden_grads(p, l):
+        count = 4 * capacity
+        at = pl.ds(pl.multiple_of(p * count, count), count)
+        weight_part = jnp.zeros((count, 1), jnp.float32)
+        for j in range(pieces):
+            cut = slice(j * width, (j + 1) * width)
+            grad = dot_nt(rows_own[l], down[l, cut, pl.ds(own_at, features)])
+            grad = grad + dot_nt(rows_other[l], down[l, cut, pl.ds(other_at, features)])
+            gate = gate_ref[l, at, cut].astype(jnp.float32)
+            up = up_ref[l, at, cut].astype(jnp.float32)
+            sigmoid = jax.nn.sigmoid(gate)
+            active = gate * sigmoid
+            weight_part = weight_part + jnp.sum(grad * active * up, axis=1, keepdims=True)
+            scaled = scale[l][:, :1] * grad
+            grad_gate = scaled * up * sigmoid * (1.0 + gate * (1.0 - sigmoid))
+            hidden_ref[l, at, cut] = grad_gate.astype(jnp.bfloat16)
+            cut = slice(hidden + j * width, hidden + (j + 1) * width)
+            hidden_ref[l, at, cut] = (scaled * active).astype(jnp.bfloat16)
+        weight_part = weight_part.astype(jnp.bfloat16).astype(jnp.float32)
+        for q in range(4):
+            b = p * 4 + q
+            pick = one_hot(slot_ref[b, pl.ds(l, 1)], capacity)
+            piece = weight_part[q * capacity : (q + 1) * capacity]
+            part_ref[b, pl.ds(l, 1)] = jnp.sum(pick * piece, axis=0, keepdims=True)
+
+    @pl.loop(0, nz)
+    def _(k):
+        p = order(k)
+        mine = index(p, y, x)
+        side, over = index(p, y, 1 - x), index(p, 1 - y, x)
+        corner = index(p, 1 - y, 1 - x)
+        along_x(side, 0, p, 0).wait_recv()
+        along_y(side, 0, p, 2).start()
+        along_y(over, 1, p, 1).wait_recv()
+        along_x(over, 1, p, 2).start()
+
+        far = k + 1
+
+        @pl.when(z - far >= 0)
+        def _():
+            for h in range(2):
+                along_z(z - far, h, True).wait_recv()
+
+                @pl.when(z < nz - 1)
+                def _():
+                    along_z(z - far, h, True).start()
+
+        @pl.when(z + far < nz)
+        def _():
+            for h in range(2):
+                along_z(z + far, h, False).wait_recv()
+
+                @pl.when(z > 0)
+                def _():
+                    along_z(z + far, h, False).start()
+
+        @pl.when(far < nz)
+        def _():
+            after = order(far)
+            plane_send(after)
+            cross(index(after, y, x)).start()
+
+        along_x(side, 1, p, 1).wait_recv()
+        cross(side).start()
+        along_y(over, 0, p, 0).wait_recv()
+        cross(over).start()
+        along_y(corner, 0, p, 2).wait_recv()
+        along_x(corner, 1, p, 2).wait_recv()
+        cross(corner).start()
+
+        @pl.loop(0, 4)
+        def _(i):
+            q = lax.rem(i + y * 2 + x, 4)
+            cross(p * 4 + i).wait_recv()
+
+        @pl.loop(0, 4)
+        def _(q):
+            gather(p * 4 + q, q)
+
+        @pl.loop(0, per_group)
+        def _(l):
+            hidden_grads(p, l)
+
+    @pl.loop(0, nz)
+    def _(p):
+        for slot in range(3):
+            along_x(e, 0, p, slot).wait_send()
+            along_y(e, 0, p, slot).wait_send()
+
+        @pl.when((p <= z) & (z < nz - 1))
+        def _():
+            for h in range(2):
+                along_z(p, h, True).wait_send()
+
+        @pl.when((p >= z) & (z > 0))
+        def _():
+            for h in range(2):
+                along_z(p, h, False).wait_send()
+
+    @pl.loop(0, groups)
+    def _(b):
+        cross(b).wait_send()
+
+    @pl.loop(1, groups)
+    def _(i):
+        tile(i).wait_send()
+
+
+def combine_kernel(
+    nz, capacity,
+    hidden_hbm, slot_ref, part_ref, gate_hbm, up_hbm,
+    out_ref, part_out,
+    hid, gate, up, partial, mine_buf, send_buf, peer, from_x, from_y, from_z, part_peer, part_sum,
+    load_sem, sx, rx, sy, ry, sz, rz, sc, rc, sw, rw, sp, rp,
+):
+    e, c, z, y, x = place()
+    groups = nz * 4
+    per_group, model, hidden = gate.shape
+    tokens = slot_ref.shape[2]
+    features = mine_buf.shape[3]
+    half = tokens // 2
+    width = 512 if model % 512 == 0 else 256
+    beside, above = index(z, y, 1 - x), index(z, 1 - y, x)
+
+    loads = []
+    for l in range(per_group):
+        for i, (src, dst) in enumerate(((hidden_hbm, hid), (gate_hbm, gate), (up_hbm, up))):
+            copy = pltpu.make_async_copy(src.at[l], dst.at[l], load_sem.at[l, i])
+            copy.start()
+            loads.append(copy)
+    enter(groups, e, c)
+    part_copy = remote(part_ref, part_peer, sp, rp, e, 1 - c)
+    part_copy.start()
+
+    def order(k):
+        low = jnp.where(k < nz - 1 - z, nz - 1 - k, k - (nz - 1 - z))
+        high = jnp.where(k < z, k, nz - 1 - (k - z))
+        p = jnp.where(z < nz // 2, low, high)
+        return jnp.where(k == nz - 1, z, p)
+
+    def cross(b):
+        return remote(send_buf.at[b], peer.at[b], sc.at[b], rc.at[b], e, 1 - c)
+
+    def along_x(b, h, p, slot):
+        return remote(mine_buf.at[b, h], from_x.at[p, slot], sx.at[p, slot], rx.at[p, slot], beside, c)
+
+    def along_y(b, h, p, slot):
+        return remote(mine_buf.at[b, h], from_y.at[p, slot], sy.at[p, slot], ry.at[p, slot], above, c)
+
+    def along_z(p, h, up_way):
+        b = index(p, y, x)
+        d = 0 if up_way else 1
+        to = e + 4 if up_way else e - 4
+        return remote(mine_buf.at[b, h], from_z.at[p, d, h], sz.at[p, d, h], rz.at[p, d, h], to, c)
+
+    own_at = c * features
+    other_at = (1 - c) * features
+
+    def add(b, h, *terms):
+        total = mine_buf[b, h].astype(jnp.float32)
+        for term in terms:
+            total = total + term.astype(jnp.float32)
+        mine_buf[b, h] = total.astype(jnp.bfloat16)
+
+    def compute(p):
+        count = 4 * capacity
+        at = pl.ds(pl.multiple_of(p * count, count), count)
+
+        for l in range(per_group):
+            @pl.loop(0, model // width)
+            def _(n):
+                cut = pl.ds(pl.multiple_of(n * width, width), width)
+                got = dot_nt(hid[l, at, :hidden], gate[l, cut])
+                got = got + dot_nt(hid[l, at, hidden:], up[l, cut])
+                got = got.astype(jnp.bfloat16)
+                for q in range(4):
+                    partial[q, l * capacity : (l + 1) * capacity, cut] = got[q * capacity : (q + 1) * capacity]
+
+        def back(q, start, store):
+            b = p * 4 + q
+            slots = slot_ref[b]
+            pick = jnp.concatenate([one_hot(slots[l : l + 1], capacity) for l in range(per_group)], axis=0)
+            pick = pick.astype(jnp.bfloat16)
+            step = 256
+            for n in range(features // step):
+                cut = pl.ds(pl.multiple_of(start + n * step, 128), step)
+                got = lax.dot_general(pick, partial[q, :, cut], TN, preferred_element_type=jnp.float32)
+                store(b, n, step, got)
+
+        def store_send(b, n, step, got):
+            got = got.astype(jnp.bfloat16)
+            for h in range(2):
+                send_buf[b, h, :, n * step : (n + 1) * step] = got[h * half : (h + 1) * half]
+
+        def store_mine(b, n, step, got):
+            got = got.astype(jnp.bfloat16)
+            for h in range(2):
+                mine_buf[b, h, :, n * step : (n + 1) * step] = got[h * half : (h + 1) * half]
+
+        @pl.loop(0, 4)
+        def _(q):
+            back(q, other_at, store_send)
+            cross(p * 4 + q).start()
+
+        @pl.loop(0, 4)
+        def _(q):
+            back(q, own_at, store_mine)
+
+        @pl.loop(0, 4)
+        def _(q):
+            b = p * 4 + q
+            cross(b).wait_recv()
+            for h in range(2):
+                add(b, h, peer[b, h])
+
+    def relay(p):
+        side, over = index(p, y, 1 - x), index(p, 1 - y, x)
+        along_x(side, 0, p, 0).wait_recv()
+        add(over, 0, from_x[p, 0])
+        along_y(over, 0, p, 1).start()
+        along_y(over, 1, p, 0).wait_recv()
+        add(side, 1, from_y[p, 0])
+        along_x(side, 1, p, 2).start()
+
+    def plane_send(p):
+        side, over = index(p, y, 1 - x), index(p, 1 - y, x)
+        corner = index(p, 1 - y, 1 - x)
+        along_x(corner, 0, p, 0).start()
+        along_y(corner, 1, p, 0).start()
+        along_x(side, 0, p, 1).start()
+        along_y(over, 1, p, 2).start()
+
+    def gather(p):
+        b = index(p, y, x)
+        along_x(b, 0, p, 1).wait_recv()
+        along_y(b, 0, p, 1).wait_recv()
+        add(b, 0, from_x[p, 1], from_y[p, 1])
+        along_x(b, 1, p, 2).wait_recv()
+        along_y(b, 1, p, 2).wait_recv()
+        add(b, 1, from_x[p, 2], from_y[p, 2])
+
+        @pl.when((p > z) & (z == 0))
+        def _():
+            for h in range(2):
+                along_z(p, h, True).start()
+
+        @pl.when((p < z) & (z == nz - 1))
+        def _():
+            for h in range(2):
+                along_z(p, h, False).start()
+
+    def forward(p):
+        b = index(p, y, x)
+
+        @pl.when((p > z) & (z > 0))
+        def _():
+            for h in range(2):
+                along_z(p, h, True).wait_recv()
+                add(b, h, from_z[p, 0, h])
+                along_z(p, h, True).start()
+
+        @pl.when((p < z) & (z < nz - 1))
+        def _():
+            for h in range(2):
+                along_z(p, h, False).wait_recv()
+                add(b, h, from_z[p, 1, h])
+                along_z(p, h, False).start()
+
+    def tile(i):
+        to = lax.rem(e + i, groups)
+        return remote(part_sum.at[to], part_out.at[e], sw.at[i], rw.at[i], to, c)
+
+    @pl.loop(0, nz + 1)
+    def _(k):
+        @pl.when(k == 0)
+        def _():
+            for copy in loads:
+                copy.wait()
+
+        @pl.when(k < nz)
+        def _():
+            compute(order(k))
+
+        @pl.when(k == 0)
+        def _():
+            part_copy.wait_recv()
+            part_sum[...] = part_ref[...] + part_peer[...]
+            part_out[e] = part_sum[e]
+
+            @pl.loop(1, groups)
+            def _(i):
+                tile(i).start()
+
+        @pl.when(k >= 1)
+        def _():
+            relay(order(k - 1))
+
+        @pl.when(k < nz)
+        def _():
+            plane_send(order(k))
+
+        @pl.when(k >= 1)
+        def _():
+            gather(order(k - 1))
+
+        @pl.when((k >= 2) & (k < nz))
+        def _():
+            forward(order(k - 2))
+
+        @pl.when((k == nz - 1) & (k >= 1))
+        def _():
+            forward(order(k - 1))
+
+    mine = index(z, y, x)
+    out_ref[...] = mine_buf[mine]
+
+    @pl.when(z > 0)
+    def _():
+        for h in range(2):
+            along_z(z, h, True).wait_recv()
+            out_ref[h] = (out_ref[h].astype(jnp.float32) + from_z[z, 0, h].astype(jnp.float32)).astype(jnp.bfloat16)
+
+    @pl.when(z < nz - 1)
+    def _():
+        for h in range(2):
+            along_z(z, h, False).wait_recv()
+            out_ref[h] = (out_ref[h].astype(jnp.float32) + from_z[z, 1, h].astype(jnp.float32)).astype(jnp.bfloat16)
+
+    @pl.loop(1, groups)
+    def _(i):
+        tile(i).wait()
+
+    part_copy.wait_send()
+
+    @pl.loop(0, nz)
+    def _(p):
+        for slot in range(3):
+            along_x(e, 0, p, slot).wait_send()
+            along_y(e, 0, p, slot).wait_send()
+
+        @pl.when((p > z) & (z < nz - 1))
+        def _():
+            for h in range(2):
+                along_z(p, h, True).wait_send()
+
+        @pl.when((p < z) & (z > 0))
+        def _():
+            for h in range(2):
+                along_z(p, h, False).wait_send()
+
+    @pl.loop(0, groups)
+    def _(b):
+        cross(b).wait_send()
+
+
+def with_kernels(
+    grad_out, combine, expert_ids, saved_gate, saved_up, gate_weight, up_weight, down_weight
+):
+    groups = lax.axis_size("expert")
+    nz = groups // 4
+    per_group, model, hidden = gate_weight.shape
+    tokens, features = grad_out.shape
+    capacity = saved_gate.shape[0] // groups
+    experts = groups * per_group
+    half = tokens // 2
+    slots = groups * capacity
+    chosen = expert_ids[:, :, None] == jnp.arange(experts, dtype=jnp.int32)[None, None, :]
+    weights = jnp.sum(jnp.where(chosen, combine[:, :, None].astype(jnp.float32), 0.0), axis=1)
+    weights = weights.reshape(tokens, groups, per_group).transpose(1, 2, 0)
+    weights = jnp.pad(weights, ((0, 0), (0, ROWS - per_group), (0, 0)))
+    gate_value = saved_gate.transpose(1, 0, 2)
+    up_value = saved_up.transpose(1, 0, 2)
+    vmem = pl.BlockSpec(memory_space=pltpu.VMEM)
+    hbm = pl.BlockSpec(memory_space=pltpu.HBM)
+    bf16, f32 = jnp.bfloat16, jnp.float32
+    dma = pltpu.SemaphoreType.DMA
+    hid, slot, part = pl.pallas_call(
+        functools.partial(dispatch_kernel, nz, capacity),
+        name="dispatch",
+        out_shape=(
+            jax.ShapeDtypeStruct((per_group, slots, 2 * hidden), bf16),
+            jax.ShapeDtypeStruct((groups, ROWS, tokens), f32),
+            jax.ShapeDtypeStruct((groups, ROWS, tokens), f32),
+        ),
+        in_specs=[hbm, vmem, hbm, vmem, vmem],
+        out_specs=(vmem, vmem, vmem),
+        scratch_shapes=[
+            pltpu.VMEM((groups, 2, half, features), bf16),
+            pltpu.VMEM((groups, 2, half, features), bf16),
+            pltpu.VMEM((groups, ROWS, tokens), f32),
+            pltpu.VMEM((per_group, hidden, model), bf16),
+            pltpu.VMEM((per_group, 4 * capacity, features), bf16),
+            pltpu.VMEM((per_group, 4 * capacity, features), bf16),
+            pltpu.VMEM((per_group, 4 * capacity, 128), f32),
+            dma((2,)),
+            dma((nz, 3)), dma((nz, 3)), dma((nz, 3)), dma((nz, 3)),
+            dma((nz, 2)), dma((nz, 2)), dma((nz, 2)),
+            dma((groups,)), dma((groups,)), dma((groups,)), dma((groups,)),
+        ],
+        compiler_params=pltpu.CompilerParams(
+            collective_id=0, has_side_effects=True, vmem_limit_bytes=VMEM_LIMIT
+        ),
+    )(grad_out.reshape(2, half, features), weights, down_weight, gate_value, up_value)
+    grad_tokens, parts = pl.pallas_call(
+        functools.partial(combine_kernel, nz, capacity),
+        name="combine",
+        out_shape=(
+            jax.ShapeDtypeStruct((2, half, features), bf16),
+            jax.ShapeDtypeStruct((groups, ROWS, tokens), f32),
+        ),
+        in_specs=[hbm, vmem, vmem, hbm, hbm],
+        out_specs=(vmem, vmem),
+        scratch_shapes=[
+            pltpu.VMEM((per_group, slots, 2 * hidden), bf16),
+            pltpu.VMEM((per_group, model, hidden), bf16),
+            pltpu.VMEM((per_group, model, hidden), bf16),
+            pltpu.VMEM((4, per_group * capacity, model), bf16),
+            pltpu.VMEM((groups, 2, half, features), bf16),
+            pltpu.VMEM((groups, 2, half, features), bf16),
+            pltpu.VMEM((groups, 2, half, features), bf16),
+            pltpu.VMEM((nz, 3, half, features), bf16),
+            pltpu.VMEM((nz, 3, half, features), bf16),
+            pltpu.VMEM((nz, 2, 2, half, features), bf16),
+            pltpu.VMEM((groups, ROWS, tokens), f32),
+            pltpu.VMEM((groups, ROWS, tokens), f32),
+            dma((per_group, 3)),
+            dma((nz, 3)), dma((nz, 3)), dma((nz, 3)), dma((nz, 3)),
+            dma((nz, 2, 2)), dma((nz, 2, 2)),
+            dma((groups,)), dma((groups,)), dma((groups,)), dma((groups,)),
+            dma(()), dma(()),
+        ],
+        compiler_params=pltpu.CompilerParams(
+            collective_id=1, has_side_effects=True, vmem_limit_bytes=VMEM_LIMIT
+        ),
+    )(hid, slot, part, gate_weight, up_weight)
+    parts = parts[:, :per_group].transpose(2, 0, 1).reshape(tokens, 1, experts)
+    grad_combine = jnp.sum(jnp.where(chosen, parts, 0.0), axis=2).astype(jnp.bfloat16)
+    return grad_tokens.reshape(tokens, features), grad_combine
+
+
+def with_collectives(
     grad_out, combine, expert_ids, saved_gate, saved_up, gate_weight, up_weight, down_weight
 ):
     groups = lax.axis_size("expert")
@@ -73,6 +674,14 @@
     return (grad_tokens, grad_combine)
 
 
+def on_device(grad_out, *rest):
+    groups = lax.axis_size("expert")
+    held = 4 * groups * grad_out.size
+    if groups % 4 == 0 and lax.axis_size("etp") == 2 and held <= TOKEN_BYTES:
+        return with_kernels(grad_out, *rest)
+    return with_collectives(grad_out, *rest)
+
+
 def solution(mesh):
     in_specs = (
         P("expert", "etp"),

time: 414 us -> 181 us (0.44)
  waiting for transfers between devices: 282 us -> 0 us
  Pallas kernels: 0 us -> 170 us
  matrix products: 79.7 us -> 0 us
  blocking collectives: 16.6 us -> 0 us
  between operations: 13.9 us -> 0.66 us
  other arithmetic: 10.5 us -> 2 us
    pallas_call x0 -> x2, Pallas kernels: none -> 170 us  [the longest x1 89.3 us: with_kernels(): pl.pallas_call(functools.partial(combine_kernel, nz, capacity), name='com...]
    reduce_scatter x2 -> x0, waiting for transfers between devices: 166 us -> none  [the longest x1 143 us: on_device(): lax.psum_scatter(partial, 'expert', scatter_dimension=0, tiled=True)]
    all_gather x2 -> x0, waiting for transfers between devices: 115 us -> none  [the longest x1 108 us: on_device(): rows = lax.all_gather(grad_out, 'expert', axis=0, tiled=True)]
    dot_general x5 -> x0, matrix products: 79.7 us -> none  [the longest x1 25 us: on_device(): jnp.einsum('blct,lbcd->btd', select, partial.astype(jnp.bfloat16), prefer...]
    all_to_all x1 -> x0, blocking collectives: 14 us -> none  [on_device(): lax.all_to_all(weight_tok, 'expert', split_axis=0, concat_axis=0, tiled=T...]
    convert_element_type x7 -> x1, other arithmetic: 8.14 us -> 0.68 us  [with_kernels(): combine[:, :, None].astype(jnp.float32)]
    convert_element_type x2 -> x0, local copies, waits for them, and re-layouts: 6.02 us -> none  [the longest x1 3.11 us: on_device(): gate_value = gate_value.astype(jnp.float32)]
    transpose x1, local copies, waits for them, and re-layouts: 0.01 us -> 4.89 us  [with_kernels(): up_value = saved_up.transpose(1, 0, 2)]
  transfers between devices with their start and end apart: 5 -> 0, of which waited for: 4 -> 0; matrix products, arithmetic and copies ran while one was open for 4% -> 0% of each run, Pallas kernels for 0% -> 0%
where the time goes in v1:
time: 181 us
  Pallas kernels  170 us (94%)
  local copies, waits for them, and re-layouts  8.2 us (5%)
  other arithmetic  2 us (1%)
    pallas_call x1, Pallas kernels, with_kernels(): pl.pallas_call(functools.partial(combine_kernel, nz, capacity), name='com...  89.3 us
    pallas_call x1, Pallas kernels, with_kernels(): pl.pallas_call(functools.partial(dispatch_kernel, nz, capacity), name='di...  80.7 us
    transpose x1, local copies, waits for them, and re-layouts, with_kernels(): up_value = saved_up.transpose(1, 0, 2)  4.89 us

profile of v1, /device:TPU:0, one launch (start us, length us, event | category | flops | bytes accessed | tf_op | source)
XLA Modules:
  0.0 180.8 jit_solution(8449227846911717837)
XLA Ops:
  0.6 0.7 convert_element_type.9
  1.3 0.7 select_reduce_fusion.1
  2.0 0.6 pad.4.weights_ref
  2.7 4.9 %copy_bitcast_fusion = (bf16[2,1024,512]{2,1,0:T(8,128)(2,1)}, bf16[2,1024,512]{2,1,0:T(8,128)(2,1)}) fusion(bf16[1024,2,512]{2,1,0:T(2,128)(2,1)} %param.12, bf16[1024,2,512]{2,1,0:T(2,128)(2,1)} %param.11), kind=kLoop, calls=%fused_computation | loop fusion | bytes 8388608 | tf_op jit(solution)/shard_map/transpose | solution.py:539
  7.6 80.7 %dispatch.1 = (bf16[2,1024,1024]{2,1,0:T(8,128)(2,1)}, f32[16,8,128]{2,1,0:T(8,128)}, f32[16,8,128]{2,1,0:T(8,128)}) custom-call(bf16[2,64,1792]{2,1,0:T(8,128)(2,1)} %bitcast.13, f32[16,8,128]{2,1,0:T(8,128)} %pad.4.weights_ref, bf16[2,512,3584]{2,1,0:T(8,128)(2,1)} %down_hbm.1, bf16[2,1024,512]{2,1,0:T(8,128)(2,1)} %get-tuple-element.13.gate_ref, ...), custom_call_target="tpu_custom_call" | custom-call | tf_op jit(solution)/shard_map/dispatch/pallas_call | solution.py:544
  88.2 0.0 copy-start
  88.2 89.3 %combine.1 = (bf16[2,64,1792]{2,1,0:T(8,128)(2,1)}, f32[16,8,128]{2,1,0:T(8,128)}) custom-call(bf16[2,1024,1024]{2,1,0:T(8,128)(2,1)} %get-tuple-element.7.hidden_hbm, f32[16,8,128]{2,1,0:T(8,128)} %get-tuple-element.8.slot_ref, f32[16,8,128]{2,1,0:T(8,128)} %get-tuple-element.9.part_ref, bf16[2,3584,512]{2,1,0:T(8,128)(2,1)} %gate_hbm.1, ...), custom_call_target="tpu_custom_call" | custom-call | tf_op jit(solution)/shard_map/combine/pallas_call | solution.py:571
  177.5 0.8 slice.3
  178.4 0.0 copy-done
  178.4 0.6 select_reduce_fusion
  179.0 1.8 %copy.20 = bf16[128,1792]{1,0:T(8,128)(2,1)} copy(bf16[128,1792]{1,0:T(8,128)(2,1)} %bitcast.12) | data formatting | bytes 917504
Async XLA Ops:
  88.2 90.2 %copy-start = (s32[128,8]{0,1:T(8,128)S(1)}, s32[128,8]{0,1:T(8,128)}, u32[]{:S(2)}) copy-start(s32[128,8]{0,1:T(8,128)} %param.10) | copy-start | bytes 12292

commit v2 on v0

--- a/solution.py
+++ b/solution.py
@@ -1,10 +1,741 @@
+import functools
+
 import jax
 import jax.numpy as jnp
 from jax import lax
+from jax.experimental import pallas as pl
+from jax.experimental.pallas import tpu as pltpu
 from jax.sharding import PartitionSpec as P
 
-
-def on_device(
+MESH = pl.DeviceIdType.MESH
+VMEM_LIMIT = 67_043_328
+TOKEN_BYTES = 24 * 2**20
+NT = (((1,), (1,)), ((), ()))
+TN = (((0,), (0,)), ((), ()))
+ROWS = 8
+
+
+def dot_nt(a, b):
+    return lax.dot_general(a, b, NT, preferred_element_type=jnp.float32)
+
+
+def place():
+    e = lax.axis_index("expert")
+    c = lax.axis_index("etp")
+    return e, c, e // 4, (e // 2) % 2, e % 2
+
+
+def index(z, y, x):
+    return z * 4 + y * 2 + x
+
+
+def enter(groups, e, c):
+    barrier = pltpu.get_barrier_semaphore()
+
+    @pl.loop(1, groups)
+    def _(i):
+        pl.semaphore_signal(
+            barrier, inc=1, device_id=(lax.rem(e + i, groups), c), device_id_type=MESH
+        )
+
+    pl.semaphore_signal(barrier, inc=1, device_id=(e, 1 - c), device_id_type=MESH)
+    pl.semaphore_wait(barrier, groups)
+
+
+def remote(src, dst, send, recv, expert, core):
+    return pltpu.make_async_remote_copy(
+        src_ref=src,
+        dst_ref=dst,
+        send_sem=send,
+        recv_sem=recv,
+        device_id=(expert, core),
+        device_id_type=MESH,
+    )
+
+
+def one_hot(slot_row, capacity):
+    tokens = slot_row.shape[1]
+    at = lax.broadcasted_iota(jnp.int32, (capacity, tokens), 0).astype(jnp.float32)
+    return jnp.where(slot_row == at, 1.0, 0.0)
+
+
+def fused_kernel(
+    nz, capacity, ra, rr,
+    x_hbm, weights_ref, down_hbm, gate_hbm, up_hbm, saved_gate_hbm, saved_up_hbm,
+    out_ref, part_out,
+    own, other, mine, send, weights, slots_at, part, part_peer, part_sum,
+    down, gate, up, work, hid, scale, saved_gate, saved_up, from_x, from_y, from_zc, from_zr,
+    load_sem, saved_sem,
+    asx, arx, asy, ary, asu, asd, arz, aru, ard, arr, acs, acr, sw, rw,
+    rsx, rrx, rsy, rry, zcs, zcr, zrs, zrr, bcs, bcr, sp, rp, qs, qr, credit,
+):
+    e, c, z, y, x = place()
+    groups = nz * 4
+    per_group, hidden, model = down.shape
+    tokens = weights.shape[2]
+    half, features = own.shape[2:]
+    width = 256
+    pieces = hidden // width
+    count = 4 * capacity
+    beside, above = index(z, y, 1 - x), index(z, 1 - y, x)
+    whole = pl.ds(0, half)
+    tail = pl.ds(ra, half - ra)
+
+    load_x = pltpu.make_async_copy(x_hbm, own.at[e], load_sem.at[0])
+    load_x.start()
+    loads = [
+        pltpu.make_async_copy(src, dst, load_sem.at[i + 1])
+        for i, (src, dst) in enumerate(((down_hbm, down), (gate_hbm, gate), (up_hbm, up)))
+    ]
+
+    def order(k):
+        low = jnp.where(k <= z, z - k, k)
+        back = nz - 1 - z
+        high = jnp.where(k <= back, z + k, nz - 1 - k)
+        return jnp.where(z < nz // 2, low, high)
+
+    def passing(i):
+        low = jnp.where(i < nz - 1 - z, z + 1 + i, nz - 2 - i)
+        high = jnp.where(i < z, z - 1 - i, i + 1)
+        return jnp.where(z < nz // 2, low, high)
+
+    def load_saved(p):
+        at = pl.ds(pl.multiple_of(p * count, count), count)
+        return [
+            pltpu.make_async_copy(saved_gate_hbm.at[:, at], saved_gate, saved_sem.at[0]),
+            pltpu.make_async_copy(saved_up_hbm.at[:, at], saved_up, saved_sem.at[1]),
+        ]
+
+    weights[e] = weights_ref[e]
+    enter(groups, e, c)
+
+    def a_x(b, h, p, slot, rows):
+        at = own.at[b, h, rows]
+        return remote(at, at, asx.at[p, slot], arx.at[p, slot], beside, c)
+
+    def a_y(b, h, p, slot, rows):
+        at = own.at[b, h, rows]
+        return remote(at, at, asy.at[p, slot], ary.at[p, slot], above, c)
+
+    def a_z(p, h, up_way):
+        at = own.at[index(p, y, x), h]
+        sems = asu if up_way else asd
+        return remote(at, at, sems.at[p, h], arz.at[p, h], e + 4 if up_way else e - 4, c)
+
+    def others(p):
+        return index(p, y, 1 - x), index(p, 1 - y, x), index(p, 1 - y, 1 - x)
+
+    def a_r(p, j, up_way):
+        at = own.at[others(p)[j], :, pl.ds(0, ra)]
+        sems = aru if up_way else ard
+        return remote(at, at, sems.at[p, j], arr.at[p, j], e + 4 if up_way else e - 4, c)
+
+    def cross(b):
+        return remote(own.at[b], other.at[b], acs.at[b], acr.at[b], e, 1 - c)
+
+    def a_send(p, rows):
+        b = index(p, y, x)
+        a_x(b, 0, p, 0, rows).start()
+        a_y(b, 1, p, 1, rows).start()
+        a_x(b, 1, p, 1, rows).start()
+        a_y(b, 0, p, 0, rows).start()
+
+    def a_relay(p, rows):
+        side, over, _ = others(p)
+        a_x(side, 0, p, 0, rows).wait_recv()
+        a_y(side, 0, p, 2, rows).start()
+        a_y(over, 1, p, 1, rows).wait_recv()
+        a_x(over, 1, p, 2, rows).start()
+
+    def a_arrive(far):
+        @pl.when(z - far >= 0)
+        def _():
+            for h in range(2):
+                a_z(z - far, h, True).wait_recv()
+
+                @pl.when(z < nz - 1)
+                def _():
+                    a_z(z - far, h, True).start()
+
+        @pl.when(z + far < nz)
+        def _():
+            for h in range(2):
+                a_z(z + far, h, False).wait_recv()
+
+                @pl.when(z > 0)
+                def _():
+                    a_z(z + far, h, False).start()
+
+        @pl.when(far < nz)
+        def _():
+            after = order(far)
+            a_send(after, tail)
+            cross(index(after, y, x)).start()
+
+    def a_spread(j):
+        @pl.when(z < nz - 1)
+        def _():
+            a_r(z, j, True).start()
+
+        @pl.when(z > 0)
+        def _():
+            a_r(z, j, False).start()
+
+    def a_finish_own():
+        side, over, corner = others(z)
+        a_x(side, 1, z, 1, whole).wait_recv()
+        a_spread(0)
+        cross(side).start()
+        a_y(over, 0, z, 0, whole).wait_recv()
+        a_spread(1)
+        cross(over).start()
+        a_y(corner, 0, z, 2, whole).wait_recv()
+        a_x(corner, 1, z, 2, whole).wait_recv()
+        a_spread(2)
+        cross(corner).start()
+
+    def a_finish(k, p):
+        @pl.when(z - k >= 0)
+        def _():
+            for j in range(3):
+                a_r(z - k, j, True).wait_recv()
+
+                @pl.when(z < nz - 1)
+                def _():
+                    a_r(z - k, j, True).start()
+
+        @pl.when(z + k < nz)
+        def _():
+            for j in range(3):
+                a_r(z + k, j, False).wait_recv()
+
+                @pl.when(z > 0)
+                def _():
+                    a_r(z + k, j, False).start()
+
+        side, over, corner = others(p)
+        a_x(side, 1, p, 1, tail).wait_recv()
+        cross(side).start()
+        a_y(over, 0, p, 0, tail).wait_recv()
+        cross(over).start()
+        a_y(corner, 0, p, 2, tail).wait_recv()
+        a_x(corner, 1, p, 2, tail).wait_recv()
+        cross(corner).start()
+
+    def tile(i):
+        to = lax.rem(e + i, groups)
+        return remote(weights_ref.at[to], weights.at[e], sw.at[i], rw.at[i], to, c)
+
+    own_at = c * features
+    other_at = (1 - c) * features
+
+    def apart(first, second):
+        none = jnp.zeros_like(first)
+        upper = jnp.concatenate([first, none], axis=1)
+        lower = jnp.concatenate([none, second], axis=1)
+        return jnp.concatenate([upper, lower], axis=0).astype(jnp.bfloat16)
+
+    def picks_of(b):
+        slots = slots_at[b]
+        return [one_hot(slots[l : l + 1], capacity) for l in range(per_group)]
+
+    def gather(p, i):
+        both = []
+        for j in range(2):
+            b, q = p * 4 + 2 * i + j, 2 * i + j
+            table = weights[b]
+            picks = picks_of(b)
+            for l in range(per_group):
+                amount = jnp.sum(picks[l] * table[l : l + 1], axis=1, keepdims=True)
+                scale[l, pl.ds(q * capacity, capacity)] = jnp.broadcast_to(amount, (capacity, 128))
+            both.append(jnp.concatenate(picks, axis=0))
+        pick = apart(*both)
+        for s, held in ((0, own), (1, other)):
+            block = held[pl.ds(p * 4 + 2 * i, 2)].reshape(2 * tokens, features)
+            got = jnp.dot(pick, block, preferred_element_type=jnp.float32).astype(jnp.bfloat16)
+            for j in range(2):
+                for l in range(per_group):
+                    at = (j * per_group + l) * capacity
+                    to = l * count + (2 * i + j) * capacity
+                    work[s, pl.ds(to, capacity)] = got[at : at + capacity]
+
+    def hidden_grads(p, l):
+        weight_part = jnp.zeros((count, 1), jnp.float32)
+        at = pl.ds(pl.multiple_of(l * count, count), count)
+        for j in range(pieces):
+            cut = slice(j * width, (j + 1) * width)
+            grad = dot_nt(work[0, at], down[l, cut, pl.ds(pl.multiple_of(own_at, 128), features)])
+            grad = grad + dot_nt(work[1, at], down[l, cut, pl.ds(pl.multiple_of(other_at, 128), features)])
+            gate_value = saved_gate[l, :, cut].astype(jnp.float32)
+            up_value = saved_up[l, :, cut].astype(jnp.float32)
+            sigmoid = jax.nn.sigmoid(gate_value)
+            active = gate_value * sigmoid
+            weight_part = weight_part + jnp.sum(grad * active * up_value, axis=1, keepdims=True)
+            scaled = scale[l][:, :1] * grad
+            grad_gate = scaled * up_value * sigmoid * (1.0 + gate_value * (1.0 - sigmoid))
+            hid[l, :, cut] = grad_gate.astype(jnp.bfloat16)
+            cut = slice(hidden + j * width, hidden + (j + 1) * width)
+            hid[l, :, cut] = (scaled * active).astype(jnp.bfloat16)
+        weight_part = weight_part.astype(jnp.bfloat16).astype(jnp.float32)
+        for q in range(4):
+            b = p * 4 + q
+            pick = one_hot(slots_at[b, pl.ds(l, 1)], capacity)
+            piece = weight_part[q * capacity : (q + 1) * capacity]
+            part[b, pl.ds(l, 1)] = jnp.sum(pick * piece, axis=0, keepdims=True)
+
+    def back_cross(p, q):
+        return remote(send.at[q], other.at[p * 4 + q], bcs.at[q], bcr.at[q], e, 1 - c)
+
+    def front(p):
+        @pl.loop(0, 4)
+        def _(q):
+            cross(p * 4 + q).wait_recv()
+
+        @pl.loop(0, 2)
+        def _(i):
+            gather(p, i)
+
+        pl.semaphore_signal(credit, inc=1, device_id=(e, 1 - c), device_id_type=MESH)
+        for copy in load_saved(p):
+            copy.wait()
+
+        @pl.loop(0, per_group)
+        def _(l):
+            hidden_grads(p, l)
+
+    def products(s, start):
+        @pl.loop(0, per_group)
+        def _(l):
+            rows = pl.ds(pl.multiple_of(start, 128), features)
+            got = dot_nt(hid[l, :, :hidden], gate[l, rows])
+            got = got + dot_nt(hid[l, :, hidden:], up[l, rows])
+            got = got.astype(jnp.bfloat16)
+            for q in range(4):
+                at = q * per_group * capacity + l * capacity
+                work[s, pl.ds(at, capacity)] = got[q * capacity : (q + 1) * capacity]
+
+    def to_tokens(p, i, s):
+        pick = apart(*[jnp.concatenate(picks_of(p * 4 + 2 * i + j), axis=0) for j in range(2)])
+        size = 2 * per_group * capacity
+        rows = pl.ds(pl.multiple_of(i * size, size), size)
+        got = lax.dot_general(pick, work[s, rows], TN, preferred_element_type=jnp.float32)
+        return got.astype(jnp.bfloat16).reshape(2, 2, half, features)
+
+    def back(k, p):
+        products(1, other_at)
+        pl.semaphore_wait(credit, 1)
+
+        @pl.loop(0, 2)
+        def _(i):
+            for j in range(2):
+                @pl.when(k > 0)
+                def _():
+                    back_cross(p, 2 * i + j).wait_send()
+
+            send[pl.ds(2 * i, 2)] = to_tokens(p, i, 1)
+            for j in range(2):
+                back_cross(p, 2 * i + j).start()
+
+        products(0, own_at)
+
+        @pl.loop(0, 2)
+        def _(i):
+            got = to_tokens(p, i, 0)
+            for j in range(2):
+                b = p * 4 + 2 * i + j
+                back_cross(p, 2 * i + j).wait_recv()
+                mine[b] = (got[j].astype(jnp.float32) + other[b].astype(jnp.float32)).astype(jnp.bfloat16)
+
+    low = pl.ds(0, rr)
+    high = pl.ds(rr, half - rr)
+
+    def add(b, h, rows, *terms):
+        total = mine[b, h, rows].astype(jnp.float32)
+        for term in terms:
+            total = total + term.astype(jnp.float32)
+        mine[b, h, rows] = total.astype(jnp.bfloat16)
+
+    def r_x(b, h, t, slot, rows):
+        dst = from_x.at[t, slot, pl.ds(0, rows.size)]
+        return remote(mine.at[b, h, rows], dst, rsx.at[t, slot], rrx.at[t, slot], beside, c)
+
+    def r_y(b, h, t, slot, rows):
+        dst = from_y.at[t, slot, pl.ds(0, rows.size)]
+        return remote(mine.at[b, h, rows], dst, rsy.at[t, slot], rry.at[t, slot], above, c)
+
+    def landing(p, up_way):
+        return p if up_way else jnp.where(p == z - 1, nz, p)
+
+    def r_zc(p, h, up_way):
+        t = landing(p, up_way)
+        src = mine.at[index(p, y, x), h, high]
+        return remote(src, from_zc.at[t, h], zcs.at[p, h], zcr.at[t, h], e + 4 if up_way else e - 4, c)
+
+    def r_zr(p, q, up_way):
+        t = landing(p, up_way)
+        src = mine.at[p * 4 + q, :, low]
+        return remote(src, from_zr.at[t, q], zrs.at[p, q], zrr.at[t, q], e + 4 if up_way else e - 4, c)
+
+    def got_zc(t, h):
+        return remote(mine.at[e, h, high], from_zc.at[t, h], zcs.at[0, h], zcr.at[t, h], e, 1 - c)
+
+    def got_zr(t, q):
+        return remote(mine.at[q, :, low], from_zr.at[t, q], zrs.at[0, q], zrr.at[t, q], e, 1 - c)
+
+    def r_send(p, t, rows):
+        side, over, corner = others(p)
+        r_x(corner, 0, t, 0, rows).start()
+        r_y(corner, 1, t, 0, rows).start()
+        r_x(side, 0, t, 1, rows).start()
+        r_y(over, 1, t, 2, rows).start()
+
+    def r_relay(p, t, rows):
+        side, over, _ = others(p)
+        n = pl.ds(0, rows.size)
+        r_x(side, 0, t, 0, rows).wait_recv()
+        add(over, 0, rows, from_x[t, 0, n])
+        r_y(over, 0, t, 1, rows).start()
+        r_y(over, 1, t, 0, rows).wait_recv()
+        add(side, 1, rows, from_y[t, 0, n])
+        r_x(side, 1, t, 2, rows).start()
+
+    def r_gather(p, t, rows):
+        b = index(p, y, x)
+        n = pl.ds(0, rows.size)
+        for h in range(2):
+            r_x(b, h, t, h + 1, rows).wait_recv()
+            r_y(b, h, t, h + 1, rows).wait_recv()
+            add(b, h, rows, from_x[t, h + 1, n], from_y[t, h + 1, n])
+
+    def col_start(p):
+        @pl.when((p > z) & (z == 0))
+        def _():
+            for h in range(2):
+                r_zc(p, h, True).start()
+
+        @pl.when((p < z) & (z == nz - 1))
+        def _():
+            for h in range(2):
+                r_zc(p, h, False).start()
+
+    def col_pass(p):
+        b = index(p, y, x)
+
+        def go(up_way):
+            for h in range(2):
+                got_zc(p, h).wait_recv()
+                add(b, h, high, from_zc[p, h])
+                r_zc(p, h, up_way).start()
+
+        @pl.when((p > z) & (z > 0))
+        def _():
+            go(True)
+
+        @pl.when((p < z) & (z < nz - 1))
+        def _():
+            go(False)
+
+    def rows_start(p):
+        @pl.when((p > z) & (z == 0))
+        def _():
+            for q in range(4):
+                r_zr(p, q, True).start()
+
+        @pl.when((p < z) & (z == nz - 1))
+        def _():
+            for q in range(4):
+                r_zr(p, q, False).start()
+
+    def rows_add(t, q, b):
+        got_zr(t, q).wait_recv()
+        for h in range(2):
+            add(b, h, low, from_zr[t, q, h])
+
+    def rows_pass(p):
+        def go(up_way):
+            @pl.loop(0, 4)
+            def _(q):
+                rows_add(p, q, p * 4 + q)
+                r_zr(p, q, up_way).start()
+
+        @pl.when((p > z) & (z > 0))
+        def _():
+            go(True)
+
+        @pl.when((p < z) & (z < nz - 1))
+        def _():
+            go(False)
+
+    def rows_final():
+        @pl.when(z > 0)
+        def _():
+            @pl.loop(0, 4)
+            def _(q):
+                rows_add(z, q, z * 4 + q)
+
+        @pl.when(z < nz - 1)
+        def _():
+            @pl.loop(0, 4)
+            def _(q):
+                rows_add(nz, q, z * 4 + q)
+
+    @pl.loop(1, groups)
+    def _(i):
+        tile(i).start()
+
+    load_x.wait()
+    a_send(z, whole)
+    for h in range(2):
+        @pl.when(z < nz - 1)
+        def _():
+            a_z(z, h, True).start()
+
+        @pl.when(z > 0)
+        def _():
+            a_z(z, h, False).start()
+
+    cross(e).start()
+    for copy in load_saved(z):
+        copy.start()
+    for copy in loads:
+        copy.start()
+    part[...] = jnp.zeros_like(part)
+    a_relay(z, whole)
+    a_arrive(1)
+
+    @pl.loop(1, groups)
+    def _(i):
+        tile(i).wait_recv()
+
+    named = (weights[...] > 0).astype(jnp.bfloat16).reshape(groups * ROWS, tokens)
+    first = lax.broadcasted_iota(jnp.int32, (tokens, tokens), 0)
+    second = lax.broadcasted_iota(jnp.int32, (tokens, tokens), 1)
+    before = (first < second).astype(jnp.bfloat16)
+    position = jnp.dot(named, before, preferred_element_type=jnp.float32)
+    slots_at[...] = jnp.where(named > 0, position, -1.0).reshape(groups, ROWS, tokens)
+
+    @pl.loop(0, nz)
+    def _(k):
+        p = order(k)
+
+        @pl.when(k == 0)
+        def _():
+            a_finish_own()
+            for copy in loads:
+                copy.wait()
+
+        @pl.when(k > 0)
+        def _():
+            a_finish(k, p)
+
+        front(p)
+
+        @pl.when(k + 1 < nz)
+        def _():
+            for copy in load_saved(order(k + 1)):
+                copy.start()
+            a_relay(order(k + 1), tail)
+            a_arrive(k + 2)
+
+        back(k, p)
+
+        @pl.when(k > 0)
+        def _():
+            rows_start(p)
+
+        @pl.when(k == nz - 2)
+        def _():
+            @pl.loop(1, nz - 1)
+            def _(i):
+                r_send(order(i), order(i), high)
+
+    part_copy = remote(part, part_peer, sp, rp, e, 1 - c)
+    part_copy.start()
+
+    def part_tile(i):
+        to = lax.rem(e + i, groups)
+        return remote(part_sum.at[to], part_out.at[e], qs.at[i], qr.at[i], to, c)
+
+    last = order(nz - 1)
+    r_send(last, last, high)
+    for i in range(1, nz - 1):
+        r_relay(order(i), order(i), high)
+    rows_pass(passing(0))
+    r_relay(last, last, high)
+    r_send(z, z, high)
+    part_copy.wait()
+    part_sum[...] = part[...] + part_peer[...]
+    part_out[e] = part_sum[e]
+
+    @pl.loop(1, groups)
+    def _(i):
+        part_tile(i).start()
+
+    for i in range(1, nz):
+        p = order(i)
+        r_gather(p, p, high)
+        col_start(p)
+        if i < nz - 1:
+            rows_pass(passing(i))
+    rows_final()
+    r_send(z, nz, low)
+    r_relay(z, z, high)
+    for i in range(nz - 2):
+        col_pass(passing(i))
+    r_relay(z, nz, low)
+    col_pass(passing(nz - 2))
+    r_gather(z, z, high)
+    r_gather(z, nz, low)
+
+    at_home = index(z, y, x)
+    out_ref[...] = mine[at_home]
+
+    def col_final(t):
+        for h in range(2):
+            got_zc(t, h).wait_recv()
+            total = out_ref[h, high].astype(jnp.float32) + from_zc[t, h].astype(jnp.float32)
+            out_ref[h, high] = total.astype(jnp.bfloat16)
+
+    @pl.when(z > 0)
+    def _():
+        col_final(z)
+
+    @pl.when(z < nz - 1)
+    def _():
+        col_final(nz)
+
+    @pl.loop(1, groups)
+    def _(i):
+        tile(i).wait_send()
+        part_tile(i).wait()
+
+    def sent_xy(p, rows):
+        for slot in range(3):
+            a_x(e, 0, p, slot, rows).wait_send()
+            a_y(e, 0, p, slot, rows).wait_send()
+
+    sent_xy(z, whole)
+    for slot in range(3):
+        r_x(e, 0, nz, slot, low).wait_send()
+        r_y(e, 0, nz, slot, low).wait_send()
+
+    @pl.loop(0, nz)
+    def _(p):
+        @pl.when(p != z)
+        def _():
+            sent_xy(p, tail)
+
+        for slot in range(3):
+            r_x(e, 0, p, slot, high).wait_send()
+            r_y(e, 0, p, slot, high).wait_send()
+
+        @pl.when((p <= z) & (z < nz - 1))
+        def _():
+            for h in range(2):
+                a_z(p, h, True).wait_send()
+            for j in range(3):
+                a_r(p, j, True).wait_send()
+
+        @pl.when((p >= z) & (z > 0))
+        def _():
+            for h in range(2):
+                a_z(p, h, False).wait_send()
+            for j in range(3):
+                a_r(p, j, False).wait_send()
+
+        @pl.when((p > z) & (z < nz - 1))
+        def _():
+            for h in range(2):
+                r_zc(p, h, True).wait_send()
+            for q in range(4):
+                r_zr(p, q, True).wait_send()
+
+        @pl.when((p < z) & (z > 0))
+        def _():
+            for h in range(2):
+                r_zc(p, h, False).wait_send()
+            for q in range(4):
+                r_zr(p, q, False).wait_send()
+
+    @pl.loop(0, groups)
+    def _(b):
+        cross(b).wait_send()
+
+    @pl.loop(0, 4)
+    def _(q):
+        back_cross(z, q).wait_send()
+
+
+def with_kernel(
+    grad_out, combine, expert_ids, saved_gate, saved_up, gate_weight, up_weight, down_weight
+):
+    groups = lax.axis_size("expert")
+    nz = groups // 4
+    per_group, model, hidden = gate_weight.shape
+    tokens, features = grad_out.shape
+    capacity = saved_gate.shape[0] // groups
+    experts = groups * per_group
+    half = tokens // 2
+    ra = half // 64 * 16
+    rr = half // 64 * 16
+    chosen = expert_ids[:, :, None] == jnp.arange(experts, dtype=jnp.int32)[None, None, :]
+    weights = jnp.sum(jnp.where(chosen, combine[:, :, None].astype(jnp.float32), 0.0), axis=1)
+    weights = weights.reshape(tokens, groups, per_group).transpose(1, 2, 0)
+    weights = jnp.pad(weights, ((0, 0), (0, ROWS - per_group), (0, 0)))
+    gate_value = saved_gate.transpose(1, 0, 2)
+    up_value = saved_up.transpose(1, 0, 2)
+    vmem = pl.BlockSpec(memory_space=pltpu.VMEM)
+    hbm = pl.BlockSpec(memory_space=pltpu.HBM)
+    bf16, f32 = jnp.bfloat16, jnp.float32
+    dma = pltpu.SemaphoreType.DMA
+    table = pltpu.VMEM((groups, ROWS, tokens), f32)
+    blocks = pltpu.VMEM((groups, 2, half, features), bf16)
+    count = 4 * capacity
+    grad_tokens, parts = pl.pallas_call(
+        functools.partial(fused_kernel, nz, capacity, ra, rr),
+        name="experts",
+        out_shape=(
+            jax.ShapeDtypeStruct((2, half, features), bf16),
+            jax.ShapeDtypeStruct((groups, ROWS, tokens), f32),
+        ),
+        in_specs=[hbm, vmem, hbm, hbm, hbm, hbm, hbm],
+        out_specs=(vmem, vmem),
+        scratch_shapes=[
+            blocks, blocks, blocks,
+            pltpu.VMEM((4, 2, half, features), bf16),
+            table, table, table, table, table,
+            pltpu.VMEM((per_group, hidden, model), bf16),
+            pltpu.VMEM((per_group, model, hidden), bf16),
+            pltpu.VMEM((per_group, model, hidden), bf16),
+            pltpu.VMEM((2, per_group * count, features), bf16),
+            pltpu.VMEM((per_group, count, 2 * hidden), bf16),
+            pltpu.VMEM((per_group, count, 128), f32),
+            pltpu.VMEM((per_group, count, hidden), bf16),
+            pltpu.VMEM((per_group, count, hidden), bf16),
+            pltpu.VMEM((nz + 1, 3, half - rr, features), bf16),
+            pltpu.VMEM((nz + 1, 3, half - rr, features), bf16),
+            pltpu.VMEM((nz + 1, 2, half - rr, features), bf16),
+            pltpu.VMEM((nz + 1, 4, 2, rr, features), bf16),
+            dma((4,)), dma((2,)),
+            dma((nz, 3)), dma((nz, 3)), dma((nz, 3)), dma((nz, 3)),
+            dma((nz, 2)), dma((nz, 2)), dma((nz, 2)),
+            dma((nz, 3)), dma((nz, 3)), dma((nz, 3)),
+            dma((groups,)), dma((groups,)), dma((groups,)), dma((groups,)),
+            dma((nz + 1, 3)), dma((nz + 1, 3)), dma((nz + 1, 3)), dma((nz + 1, 3)),
+            dma((nz, 2)), dma((nz + 1, 2)), dma((nz, 4)), dma((nz + 1, 4)),
+            dma((4,)), dma((4,)), dma(()), dma(()), dma((groups,)), dma((groups,)),
+            pltpu.SemaphoreType.REGULAR,
+        ],
+        compiler_params=pltpu.CompilerParams(
+            collective_id=0, has_side_effects=True, vmem_limit_bytes=VMEM_LIMIT
+        ),
+    )(grad_out.reshape(2, half, features), weights, down_weight, gate_weight, up_weight, gate_value, up_value)
+    parts = parts[:, :per_group].transpose(2, 0, 1).reshape(tokens, 1, experts)
+    grad_combine = jnp.sum(jnp.where(chosen, parts, 0.0), axis=2).astype(jnp.bfloat16)
+    return grad_tokens.reshape(tokens, features), grad_combine
+
+
+def with_collectives(
     grad_out, combine, expert_ids, saved_gate, saved_up, gate_weight, up_weight, down_weight
 ):
     groups = lax.axis_size("expert")
@@ -73,6 +804,14 @@
     return (grad_tokens, grad_combine)
 
 
+def on_device(grad_out, *rest):
+    groups = lax.axis_size("expert")
+    held = 4 * groups * grad_out.size
+    if groups % 4 == 0 and lax.axis_size("etp") == 2 and held <= TOKEN_BYTES:
+        return with_kernel(grad_out, *rest)
+    return with_collectives(grad_out, *rest)
+
+
 def solution(mesh):
     in_specs = (
         P("expert", "etp"),

time: 414 us -> 148 us (0.36)
  waiting for transfers between devices: 282 us -> 0 us
  Pallas kernels: 0 us -> 136 us
  matrix products: 79.7 us -> 0 us
  blocking collectives: 16.6 us -> 0 us
  between operations: 13.9 us -> 0.64 us
  other arithmetic: 10.5 us -> 2.69 us
    reduce_scatter x2 -> x0, waiting for transfers between devices: 166 us -> none  [the longest x1 143 us: on_device(): lax.psum_scatter(partial, 'expert', scatter_dimension=0, tiled=True)]
    pallas_call x0 -> x1, Pallas kernels: none -> 136 us  [with_kernel(): pl.pallas_call(functools.partial(fused_kernel, nz, capacity, ra, rr), nam...]
    all_gather x2 -> x0, waiting for transfers between devices: 115 us -> none  [the longest x1 108 us: on_device(): rows = lax.all_gather(grad_out, 'expert', axis=0, tiled=True)]
    dot_general x5 -> x0, matrix products: 79.7 us -> none  [the longest x1 25 us: on_device(): jnp.einsum('blct,lbcd->btd', select, partial.astype(jnp.bfloat16), prefer...]
    all_to_all x1 -> x0, blocking collectives: 14 us -> none  [on_device(): lax.all_to_all(weight_tok, 'expert', split_axis=0, concat_axis=0, tiled=T...]
    convert_element_type x7 -> x1, other arithmetic: 8.14 us -> 0.68 us  [with_kernel(): combine[:, :, None].astype(jnp.float32)]
    convert_element_type x2 -> x0, local copies, waits for them, and re-layouts: 6.02 us -> none  [the longest x1 3.11 us: on_device(): gate_value = gate_value.astype(jnp.float32)]
    transpose x1, local copies, waits for them, and re-layouts: 0.01 us -> 4.85 us  [with_kernel(): up_value = saved_up.transpose(1, 0, 2)]
  transfers between devices with their start and end apart: 5 -> 0, of which waited for: 4 -> 0; matrix products, arithmetic and copies ran while one was open for 4% -> 0% of each run, Pallas kernels for 0% -> 0%
where the time goes in v2:
time: 148 us; the launch traced here: 147 us
  Pallas kernels  136 us (92%)
  local copies, waits for them, and re-layouts  8.15 us (6%)
  other arithmetic  2.69 us (2%)
    pallas_call x1, Pallas kernels, with_kernel(): pl.pallas_call(functools.partial(fused_kernel, nz, capacity, ra, rr), nam...  136 us
    transpose x1, local copies, waits for them, and re-layouts, with_kernel(): up_value = saved_up.transpose(1, 0, 2)  4.85 us

profile of v2, /device:TPU:0, one launch (start us, length us, event | category | flops | bytes accessed | tf_op | source)
XLA Modules:
  0.0 147.3 jit_solution(4698891283509645276)
XLA Ops:
  0.6 0.7 convert_element_type.9
  1.3 0.7 select_reduce_fusion.1
  2.0 0.6 pad.4.weights_ref
  2.7 4.8 %copy_bitcast_fusion = (bf16[2,1024,512]{2,1,0:T(8,128)(2,1)}, bf16[2,1024,512]{2,1,0:T(8,128)(2,1)}) fusion(bf16[1024,2,512]{2,1,0:T(2,128)(2,1)} %param.12, bf16[1024,2,512]{2,1,0:T(2,128)(2,1)} %param.11), kind=kLoop, calls=%fused_computation | loop fusion | bytes 8388608 | tf_op jit(solution)/shard_map/transpose | solution.py:686
  7.5 135.8 %experts.1 = (bf16[2,64,1792]{2,1,0:T(8,128)(2,1)}, f32[16,8,128]{2,1,0:T(8,128)}) custom-call(bf16[2,64,1792]{2,1,0:T(8,128)(2,1)} %bitcast.13, f32[16,8,128]{2,1,0:T(8,128)} %pad.4.weights_ref, bf16[2,512,3584]{2,1,0:T(8,128)(2,1)} %down_hbm.1, bf16[2,3584,512]{2,1,0:T(8,128)(2,1)} %gate_hbm.1, bf16[2,3584,512]{2,1,0:T(8,128)(2,1)} %up_hbm.1, ...), custom_call_target="tpu_custom_call" | custom-call | tf_op jit(solution)/shard_map/experts/pallas_call | solution.py:694
  143.4 0.8 slice.3
  144.2 1.3 select_reduce_fusion
  145.5 1.8 %copy.20 = bf16[128,1792]{1,0:T(8,128)(2,1)} copy(bf16[128,1792]{1,0:T(8,128)(2,1)} %bitcast.12) | data formatting | bytes 917504

commit v3 on v2

--- a/solution.py
+++ b/solution.py
@@ -148,18 +148,17 @@
         a_x(over, 1, p, 2, rows).start()
 
     def a_arrive(far):
-        @pl.when(z - far >= 0)
-        def _():
-            for h in range(2):
+        for h in range(2):
+            @pl.when(z - far >= 0)
+            def _():
                 a_z(z - far, h, True).wait_recv()
 
                 @pl.when(z < nz - 1)
                 def _():
                     a_z(z - far, h, True).start()
 
-        @pl.when(z + far < nz)
-        def _():
-            for h in range(2):
+            @pl.when(z + far < nz)
+            def _():
                 a_z(z + far, h, False).wait_recv()
 
                 @pl.when(z > 0)
@@ -239,27 +238,24 @@
         slots = slots_at[b]
         return [one_hot(slots[l : l + 1], capacity) for l in range(per_group)]
 
-    def gather(p, i):
-        both = []
+    def gather(p, i, s, held):
+        pick = apart(*[jnp.concatenate(picks_of(p * 4 + 2 * i + j), axis=0) for j in range(2)])
+        block = held[pl.ds(p * 4 + 2 * i, 2)].reshape(2 * tokens, features)
+        got = jnp.dot(pick, block, preferred_element_type=jnp.float32).astype(jnp.bfloat16)
         for j in range(2):
-            b, q = p * 4 + 2 * i + j, 2 * i + j
-            table = weights[b]
-            picks = picks_of(b)
             for l in range(per_group):
-                amount = jnp.sum(picks[l] * table[l : l + 1], axis=1, keepdims=True)
-                scale[l, pl.ds(q * capacity, capacity)] = jnp.broadcast_to(amount, (capacity, 128))
-            both.append(jnp.concatenate(picks, axis=0))
-        pick = apart(*both)
-        for s, held in ((0, own), (1, other)):
-            block = held[pl.ds(p * 4 + 2 * i, 2)].reshape(2 * tokens, features)
-            got = jnp.dot(pick, block, preferred_element_type=jnp.float32).astype(jnp.bfloat16)
-            for j in range(2):
-                for l in range(per_group):
-                    at = (j * per_group + l) * capacity
-                    to = l * count + (2 * i + j) * capacity
-                    work[s, pl.ds(to, capacity)] = got[at : at + capacity]
-
-    def hidden_grads(p, l):
+                at = (j * per_group + l) * capacity
+                to = l * count + (2 * i + j) * capacity
+                work[s, pl.ds(to, capacity)] = got[at : at + capacity]
+
+    def amounts(p, q):
+        table = weights[p * 4 + q]
+        picks = picks_of(p * 4 + q)
+        for l in range(per_group):
+            amount = jnp.sum(picks[l] * table[l : l + 1], axis=1, keepdims=True)
+            scale[l, pl.ds(q * capacity, capacity)] = jnp.broadcast_to(amount, (capacity, 128))
+
+    def hidden_grads(p, l, v):
         weight_part = jnp.zeros((count, 1), jnp.float32)
         at = pl.ds(pl.multiple_of(l * count, count), count)
         for j in range(pieces):
@@ -273,9 +269,9 @@
             weight_part = weight_part + jnp.sum(grad * active * up_value, axis=1, keepdims=True)
             scaled = scale[l][:, :1] * grad
             grad_gate = scaled * up_value * sigmoid * (1.0 + gate_value * (1.0 - sigmoid))
-            hid[l, :, cut] = grad_gate.astype(jnp.bfloat16)
+            hid[v, l, :, cut] = grad_gate.astype(jnp.bfloat16)
             cut = slice(hidden + j * width, hidden + (j + 1) * width)
-            hid[l, :, cut] = (scaled * active).astype(jnp.bfloat16)
+            hid[v, l, :, cut] = (scaled * active).astype(jnp.bfloat16)
         weight_part = weight_part.astype(jnp.bfloat16).astype(jnp.float32)
         for q in range(4):
             b = p * 4 + q
@@ -284,31 +280,39 @@
             part[b, pl.ds(l, 1)] = jnp.sum(pick * piece, axis=0, keepdims=True)
 
     def back_cross(p, q):
-        return remote(send.at[q], other.at[p * 4 + q], bcs.at[q], bcr.at[q], e, 1 - c)
-
-    def front(p):
+        t = jnp.where(p == z, 1, 0)
+        return remote(send.at[q], other.at[p * 4 + q], bcs.at[t, q], bcr.at[t, q], e, 1 - c)
+
+    def take(p):
+        @pl.loop(0, 2)
+        def _(i):
+            gather(p, i, 0, own)
+
         @pl.loop(0, 4)
         def _(q):
+            amounts(p, q)
             cross(p * 4 + q).wait_recv()
 
         @pl.loop(0, 2)
         def _(i):
-            gather(p, i)
-
-        pl.semaphore_signal(credit, inc=1, device_id=(e, 1 - c), device_id_type=MESH)
+            gather(p, i, 1, other)
+
+        pl.semaphore_signal(credit.at[p], inc=1, device_id=(e, 1 - c), device_id_type=MESH)
+
+    def grads(p, v):
         for copy in load_saved(p):
             copy.wait()
 
         @pl.loop(0, per_group)
         def _(l):
-            hidden_grads(p, l)
-
-    def products(s, start):
+            hidden_grads(p, l, v)
+
+    def products(s, start, v):
         @pl.loop(0, per_group)
         def _(l):
             rows = pl.ds(pl.multiple_of(start, 128), features)
-            got = dot_nt(hid[l, :, :hidden], gate[l, rows])
-            got = got + dot_nt(hid[l, :, hidden:], up[l, rows])
+            got = dot_nt(hid[v, l, :, :hidden], gate[l, rows])
+            got = got + dot_nt(hid[v, l, :, hidden:], up[l, rows])
             got = got.astype(jnp.bfloat16)
             for q in range(4):
                 at = q * per_group * capacity + l * capacity
@@ -321,22 +325,23 @@
         got = lax.dot_general(pick, work[s, rows], TN, preferred_element_type=jnp.float32)
         return got.astype(jnp.bfloat16).reshape(2, 2, half, features)
 
-    def back(k, p):
-        products(1, other_at)
-        pl.semaphore_wait(credit, 1)
+    def back_other(k, p, v):
+        products(1, other_at, v)
+        pl.semaphore_wait(credit.at[p], 1)
 
         @pl.loop(0, 2)
         def _(i):
             for j in range(2):
-                @pl.when(k > 0)
+                @pl.when(k > 1)
                 def _():
-                    back_cross(p, 2 * i + j).wait_send()
+                    back_cross(last, 2 * i + j).wait_send()
 
             send[pl.ds(2 * i, 2)] = to_tokens(p, i, 1)
             for j in range(2):
                 back_cross(p, 2 * i + j).start()
 
-        products(0, own_at)
+    def back_own(p, v):
+        products(0, own_at, v)
 
         @pl.loop(0, 2)
         def _(i):
@@ -366,18 +371,26 @@
     def landing(p, up_way):
         return p if up_way else jnp.where(p == z - 1, nz, p)
 
-    def r_zc(p, h, up_way):
+    links = 2 * (half // rr - 1)
+
+    def piece(i):
+        h, n = i // (half // rr - 1), lax.rem(i, half // rr - 1) + 1
+        return h, pl.ds(pl.multiple_of(n * rr, rr), rr)
+
+    def r_zc(p, i, up_way):
         t = landing(p, up_way)
-        src = mine.at[index(p, y, x), h, high]
-        return remote(src, from_zc.at[t, h], zcs.at[p, h], zcr.at[t, h], e + 4 if up_way else e - 4, c)
+        h, rows = piece(i)
+        src = mine.at[index(p, y, x), h, rows]
+        return remote(src, from_zc.at[t, i], zcs.at[p, i], zcr.at[t, i], e + 4 if up_way else e - 4, c)
 
     def r_zr(p, q, up_way):
         t = landing(p, up_way)
         src = mine.at[p * 4 + q, :, low]
         return remote(src, from_zr.at[t, q], zrs.at[p, q], zrr.at[t, q], e + 4 if up_way else e - 4, c)
 
-    def got_zc(t, h):
-        return remote(mine.at[e, h, high], from_zc.at[t, h], zcs.at[0, h], zcr.at[t, h], e, 1 - c)
+    def got_zc(t, i):
+        h, rows = piece(i)
+        return remote(mine.at[e, h, rows], from_zc.at[t, i], zcs.at[0, i], zcr.at[t, i], e, 1 - c)
 
     def got_zr(t, q):
         return remote(mine.at[q, :, low], from_zr.at[t, q], zrs.at[0, q], zrr.at[t, q], e, 1 - c)
@@ -410,22 +423,24 @@
     def col_start(p):
         @pl.when((p > z) & (z == 0))
         def _():
-            for h in range(2):
-                r_zc(p, h, True).start()
+            @pl.loop(0, links)
+            def _(i):
+                r_zc(p, i, True).start()
 
         @pl.when((p < z) & (z == nz - 1))
         def _():
-            for h in range(2):
-                r_zc(p, h, False).start()
+            @pl.loop(0, links)
+            def _(i):
+                r_zc(p, i, False).start()
 
     def col_pass(p):
-        b = index(p, y, x)
-
         def go(up_way):
-            for h in range(2):
-                got_zc(p, h).wait_recv()
-                add(b, h, high, from_zc[p, h])
-                r_zc(p, h, up_way).start()
+            @pl.loop(0, links)
+            def _(i):
+                h, rows = piece(i)
+                got_zc(p, i).wait_recv()
+                add(index(p, y, x), h, rows, from_zc[p, i])
+                r_zc(p, i, up_way).start()
 
         @pl.when((p > z) & (z > 0))
         def _():
@@ -514,40 +529,91 @@
     position = jnp.dot(named, before, preferred_element_type=jnp.float32)
     slots_at[...] = jnp.where(named > 0, position, -1.0).reshape(groups, ROWS, tokens)
 
-    @pl.loop(0, nz)
+    last = order(nz - 1)
+
+    @pl.loop(0, nz + 1)
     def _(k):
-        p = order(k)
+        p = jnp.where(k < nz, order(k), z)
+        v = jnp.where((k == 0) | (k == nz), 1, 0)
 
         @pl.when(k == 0)
         def _():
             a_finish_own()
+
+        @pl.when((k > 0) & (k < nz))
+        def _():
+            a_finish(k, p)
+
+        @pl.when(k < nz)
+        def _():
+            take(p)
+
+        @pl.when(k + 1 < nz)
+        def _():
+            a_relay(order(k + 1), tail)
+
+        @pl.when(k == 0)
+        def _():
             for copy in loads:
                 copy.wait()
 
-        @pl.when(k > 0)
-        def _():
-            a_finish(k, p)
-
-        front(p)
+        @pl.when(k < nz)
+        def _():
+            grads(p, v)
 
         @pl.when(k + 1 < nz)
         def _():
             for copy in load_saved(order(k + 1)):
                 copy.start()
-            a_relay(order(k + 1), tail)
+
+        @pl.when(k == 0)
+        def _():
+            a_arrive(2)
+
+        @pl.when(k == nz - 1)
+        def _():
+            for i in range(1, nz - 2):
+                r_gather(order(i), order(i), high)
+                col_start(order(i))
+
+        @pl.when(k == nz)
+        def _():
+            if nz > 2:
+                rows_pass(passing(0))
+
+        @pl.when(k > 0)
+        def _():
+            back_other(k, p, v)
+
+        @pl.when((k > 0) & (k + 1 < nz))
+        def _():
             a_arrive(k + 2)
 
-        back(k, p)
+        @pl.when(k == nz)
+        def _():
+            for i in range(max(nz - 2, 1), nz - 1):
+                r_gather(order(i), order(i), high)
+                col_start(order(i))
+
+        @pl.when((k > 1) & (k < nz))
+        def _():
+            r_relay(order(k - 1), order(k - 1), high)
 
         @pl.when(k > 0)
         def _():
+            back_own(p, v)
+
+        @pl.when(k == nz)
+        def _():
+            r_relay(last, last, high)
+
+        @pl.when(k > 0)
+        def _():
+            r_send(p, p, high)
+
+        @pl.when((k > 0) & (k < nz))
+        def _():
             rows_start(p)
-
-        @pl.when(k == nz - 2)
-        def _():
-            @pl.loop(1, nz - 1)
-            def _(i):
-                r_send(order(i), order(i), high)
 
     part_copy = remote(part, part_peer, sp, rp, e, 1 - c)
     part_copy.start()
@@ -556,13 +622,6 @@
         to = lax.rem(e + i, groups)
         return remote(part_sum.at[to], part_out.at[e], qs.at[i], qr.at[i], to, c)
 
-    last = order(nz - 1)
-    r_send(last, last, high)
-    for i in range(1, nz - 1):
-        r_relay(order(i), order(i), high)
-    rows_pass(passing(0))
-    r_relay(last, last, high)
-    r_send(z, z, high)
     part_copy.wait()
     part_sum[...] = part[...] + part_peer[...]
     part_out[e] = part_sum[e]
@@ -571,12 +630,11 @@
     def _(i):
         part_tile(i).start()
 
-    for i in range(1, nz):
-        p = order(i)
-        r_gather(p, p, high)
-        col_start(p)
-        if i < nz - 1:
-            rows_pass(passing(i))
+    rows_pass(passing(1 if nz > 2 else 0))
+    r_gather(last, last, high)
+    col_start(last)
+    for i in range(2, nz - 1):
+        rows_pass(passing(i))
     rows_final()
     r_send(z, nz, low)
     r_relay(z, z, high)
@@ -591,10 +649,12 @@
     out_ref[...] = mine[at_home]
 
     def col_final(t):
-        for h in range(2):
-            got_zc(t, h).wait_recv()
-            total = out_ref[h, high].astype(jnp.float32) + from_zc[t, h].astype(jnp.float32)
-            out_ref[h, high] = total.astype(jnp.bfloat16)
+        @pl.loop(0, links)
+        def _(i):
+            h, rows = piece(i)
+            got_zc(t, i).wait_recv()
+            total = out_ref[h, rows].astype(jnp.float32) + from_zc[t, i].astype(jnp.float32)
+            out_ref[h, rows] = total.astype(jnp.bfloat16)
 
     @pl.when(z > 0)
     def _():
@@ -645,15 +705,15 @@
 
         @pl.when((p > z) & (z < nz - 1))
         def _():
-            for h in range(2):
-                r_zc(p, h, True).wait_send()
+            for i in range(links):
+                r_zc(p, i, True).wait_send()
             for q in range(4):
                 r_zr(p, q, True).wait_send()
 
         @pl.when((p < z) & (z > 0))
         def _():
-            for h in range(2):
-                r_zc(p, h, False).wait_send()
+            for i in range(links):
+                r_zc(p, i, False).wait_send()
             for q in range(4):
                 r_zr(p, q, False).wait_send()
 
@@ -678,6 +738,7 @@
     half = tokens // 2
     ra = half // 64 * 16
     rr = half // 64 * 16
+    links = 2 * (half // rr - 1)
     chosen = expert_ids[:, :, None] == jnp.arange(experts, dtype=jnp.int32)[None, None, :]
     weights = jnp.sum(jnp.where(chosen, combine[:, :, None].astype(jnp.float32), 0.0), axis=1)
     weights = weights.reshape(tokens, groups, per_group).transpose(1, 2, 0)
@@ -708,13 +769,13 @@
             pltpu.VMEM((per_group, model, hidden), bf16),
             pltpu.VMEM((per_group, model, hidden), bf16),
             pltpu.VMEM((2, per_group * count, features), bf16),
-            pltpu.VMEM((per_group, count, 2 * hidden), bf16),
+            pltpu.VMEM((2, per_group, count, 2 * hidden), bf16),
             pltpu.VMEM((per_group, count, 128), f32),
             pltpu.VMEM((per_group, count, hidden), bf16),
             pltpu.VMEM((per_group, count, hidden), bf16),
             pltpu.VMEM((nz + 1, 3, half - rr, features), bf16),
             pltpu.VMEM((nz + 1, 3, half - rr, features), bf16),
-            pltpu.VMEM((nz + 1, 2, half - rr, features), bf16),
+            pltpu.VMEM((nz + 1, links, rr, features), bf16),
             pltpu.VMEM((nz + 1, 4, 2, rr, features), bf16),
             dma((4,)), dma((2,)),
             dma((nz, 3)), dma((nz, 3)), dma((nz, 3)), dma((nz, 3)),
@@ -722,9 +783,9 @@
             dma((nz, 3)), dma((nz, 3)), dma((nz, 3)),
             dma((groups,)), dma((groups,)), dma((groups,)), dma((groups,)),
             dma((nz + 1, 3)), dma((nz + 1, 3)), dma((nz + 1, 3)), dma((nz + 1, 3)),
-            dma((nz, 2)), dma((nz + 1, 2)), dma((nz, 4)), dma((nz + 1, 4)),
-            dma((4,)), dma((4,)), dma(()), dma(()), dma((groups,)), dma((groups,)),
-            pltpu.SemaphoreType.REGULAR,
+            dma((nz, links)), dma((nz + 1, links)), dma((nz, 4)), dma((nz + 1, 4)),
+            dma((2, 4)), dma((2, 4)), dma(()), dma(()), dma((groups,)), dma((groups,)),
+            pltpu.SemaphoreType.REGULAR((nz,)),
         ],
         compiler_params=pltpu.CompilerParams(
             collective_id=0, has_side_effects=True, vmem_limit_bytes=VMEM_LIMIT

time: 148 us -> 140 us (0.946)
  Pallas kernels: 136 us -> 128 us
    pallas_call x1, Pallas kernels: 136 us -> 128 us  [with_kernel(): pl.pallas_call(functools.partial(fused_kernel, nz, capacity, ra, rr), nam...]
where the time goes in v3:
time: 140 us; the launch traced here: 139 us
  Pallas kernels  128 us (91%)
  local copies, waits for them, and re-layouts  8.15 us (6%)
  other arithmetic  2.69 us (2%)
    pallas_call x1, Pallas kernels, with_kernel(): pl.pallas_call(functools.partial(fused_kernel, nz, capacity, ra, rr), nam...  128 us
    transpose x1, local copies, waits for them, and re-layouts, with_kernel(): up_value = saved_up.transpose(1, 0, 2)  4.85 us

profile of v3, /device:TPU:0, one launch (start us, length us, event | category | flops | bytes accessed | tf_op | source)
XLA Modules:
  0.0 139.2 jit_solution(11760029890200866208)
XLA Ops:
  0.6 0.7 convert_element_type.9
  1.3 0.7 select_reduce_fusion.1
  2.0 0.6 pad.4.weights_ref
  2.7 4.8 %copy_bitcast_fusion = (bf16[2,1024,512]{2,1,0:T(8,128)(2,1)}, bf16[2,1024,512]{2,1,0:T(8,128)(2,1)}) fusion(bf16[1024,2,512]{2,1,0:T(2,128)(2,1)} %param.12, bf16[1024,2,512]{2,1,0:T(2,128)(2,1)} %param.11), kind=kLoop, calls=%fused_computation | loop fusion | bytes 8388608 | tf_op jit(solution)/shard_map/transpose | solution.py:747
  7.5 127.7 %experts.1 = (bf16[2,64,1792]{2,1,0:T(8,128)(2,1)}, f32[16,8,128]{2,1,0:T(8,128)}) custom-call(bf16[2,64,1792]{2,1,0:T(8,128)(2,1)} %bitcast.13, f32[16,8,128]{2,1,0:T(8,128)} %pad.4.weights_ref, bf16[2,512,3584]{2,1,0:T(8,128)(2,1)} %down_hbm.1, bf16[2,3584,512]{2,1,0:T(8,128)(2,1)} %gate_hbm.1, bf16[2,3584,512]{2,1,0:T(8,128)(2,1)} %up_hbm.1, ...), custom_call_target="tpu_custom_call" | custom-call | tf_op jit(solution)/shard_map/experts/pallas_call | solution.py:755
  135.2 0.8 slice.3
  136.1 1.3 select_reduce_fusion
  137.4 1.8 %copy.20 = bf16[128,1792]{1,0:T(8,128)(2,1)} copy(bf16[128,1792]{1,0:T(8,128)(2,1)} %bitcast.12) | data formatting | bytes 917504
